TPU v7x, 16 devices: a 4x2x1 block of a 4x4x8 slice. The times are simulated.
16 devices in a mesh: dp: 2 (over y, z), ep: 8 (over x, core).
Axes of the slice: x: 4, y: 2, z: 1, core: 2. Of those that a mesh axis runs over, the one named last changes fastest.
The devices are a block of a 4x4x8 slice.
Arguments:
- x_rows: bfloat16 [8192, 2048], P(('dp', 'ep')), parts along dimension 0
- logits: float32 [8192, 256], P(('dp', 'ep')), parts along dimension 0
- w_in: bfloat16 [256, 2048, 512], P('ep')
- w_out: bfloat16 [256, 512, 2048], P('ep')
- shared_in: bfloat16 [2048, 512], replicated
- shared_out: bfloat16 [512, 2048], replicated
Outputs:
- output: bfloat16 [8192, 2048], P(('dp', 'ep')), parts along dimension 0
There are 2 independent parts. A program takes and returns all parts, laid end to end along the dimension named above; an argument that names none is the same for every part.
All inputs are finite; a program needn't handle non-finite values.
Results may differ from a plain program's by a relative error of at most 0.00543669.
Values are sent between devices in bfloat16 or wider.
A program may use at most 768 MiB of HBM per device.

v0:
```python
import jax
import jax.numpy as jnp
from jax import lax
from jax.sharding import PartitionSpec as P

CAP_FACTOR = 2


def expert_ffn(expert_rows, w_in, w_out):
    hidden = jax.nn.gelu(jnp.einsum("ecd,edf->ecf", expert_rows, w_in, preferred_element_type=jnp.float32)).astype(jnp.bfloat16)
    return jnp.einsum("ecf,efd->ecd", hidden, w_out, preferred_element_type=jnp.float32).astype(jnp.bfloat16)


def shared_ffn(x_rows, shared_in, shared_out):
    hidden = jax.nn.gelu(jnp.dot(x_rows, shared_in, preferred_element_type=jnp.float32)).astype(jnp.bfloat16)
    return jnp.dot(hidden, shared_out, preferred_element_type=jnp.float32).astype(jnp.bfloat16)


def solution(mesh):
    group_size = mesh.shape["ep"]

    def local_layer(x_rows, logits, w_in, w_out, shared_in, shared_out):
        tok_loc, d_model = x_rows.shape
        experts = logits.shape[1]
        num_local = experts // group_size
        capacity = tok_loc * group_size * CAP_FACTOR // experts
        pair_cap = 2 * tok_loc * CAP_FACTOR // group_size
        cand_len = min(capacity, pair_cap)
        gate_probs = jax.nn.softmax(logits, axis=-1)
        cand_score, cand_tok = lax.top_k(logits.T, cand_len)
        recv_score = lax.all_to_all(cand_score.reshape(group_size, num_local, cand_len), "ep", 0, 0)
        merged = jnp.transpose(recv_score, (1, 0, 2)).reshape(num_local, group_size * cand_len)
        chosen_pos = lax.top_k(merged, capacity)[1]
        expert_ids = jnp.arange(num_local)[:, None]
        picked = jnp.zeros((num_local, group_size * cand_len), jnp.int32).at[expert_ids, chosen_pos].set(1)
        picked_src = jnp.transpose(picked.reshape(num_local, group_size, cand_len), (1, 0, 2))
        slot_owner = jnp.cumsum(picked_src.reshape(group_size, num_local * cand_len), axis=1) - 1
        slot_by_expert = jnp.transpose(slot_owner.reshape(group_size, num_local, cand_len), (1, 0, 2)).reshape(num_local, group_size * cand_len)
        row_map = (chosen_pos // cand_len) * pair_cap + jnp.take_along_axis(slot_by_expert, chosen_pos, axis=1)
        picked_back = lax.all_to_all(picked_src.astype(jnp.float32), "ep", 0, 0)
        my_picks = picked_back.reshape(group_size, num_local * cand_len).astype(jnp.int32)
        slot_src = jnp.where(my_picks > 0, jnp.cumsum(my_picks, axis=1) - 1, pair_cap)
        owner_ids = jnp.arange(group_size)[:, None]
        cand_ids = jnp.broadcast_to(jnp.arange(num_local * cand_len), (group_size, num_local * cand_len))
        slot_cand = jnp.zeros((group_size, pair_cap), jnp.int32).at[owner_ids, slot_src].set(cand_ids, mode="drop")
        slot_tok = jnp.take_along_axis(cand_tok.reshape(group_size, num_local * cand_len), slot_cand, axis=1)
        send_rows = jnp.take(x_rows, slot_tok.reshape(-1), axis=0).reshape(group_size, pair_cap, d_model)
        recv_rows = lax.all_to_all(send_rows, "ep", 0, 0)
        expert_in = jnp.take(recv_rows.reshape(group_size * pair_cap, d_model), row_map.reshape(-1), axis=0).reshape(num_local, capacity, d_model)
        expert_out = expert_ffn(expert_in, w_in, w_out)
        back_index = jnp.zeros((group_size * pair_cap,), jnp.int32).at[row_map.reshape(-1)].set(jnp.arange(num_local * capacity))
        back_rows = jnp.take(expert_out.reshape(num_local * capacity, d_model), back_index, axis=0).reshape(group_size, pair_cap, d_model)
        returned = lax.all_to_all(back_rows, "ep", 0, 0)
        is_valid = jnp.arange(pair_cap)[None, :] < jnp.sum(my_picks, axis=1, keepdims=True)
        expert_of_slot = owner_ids * num_local + slot_cand // cand_len
        weight = jnp.where(is_valid, jnp.take(gate_probs.reshape(-1), slot_tok * experts + expert_of_slot), 0.0)
        weighted = (weight[:, :, None] * returned.astype(jnp.float32)).reshape(group_size * pair_cap, d_model)
        routed = jax.ops.segment_sum(weighted, slot_tok.reshape(-1), num_segments=tok_loc)
        summed = routed + shared_ffn(x_rows, shared_in, shared_out).astype(jnp.float32)
        return (x_rows.astype(jnp.float32) + summed).astype(jnp.bfloat16)

    row_spec = P(("dp", "ep"), None)
    expert_spec = P("ep", None, None)
    return jax.shard_map(local_layer, mesh=mesh, in_specs=(row_spec, row_spec, expert_spec, expert_spec, P(None, None), P(None, None)), out_specs=row_spec, check_vma=False)
```

profile of v0, /device:TPU:113, one launch (start us, length us, event | category | flops | bytes accessed | tf_op | source)
XLA Modules:
  0.0 456.0 jit_solution(1680255212575220167)
XLA Ops:
  0.1 15.9 %top_k.22 = (f32[256,512]{0,1:T(8,128)}, s32[256,512]{0,1:T(8,128)S(1)}) sort(f32[256,512]{0,1:T(8,128)} %bitcast.71, s32[256,512]{0,1:T(8,128)S(1)} %top_k.17.clone), dimensions={1}, to_apply=%region_0.0 | sort | flops 2228224 | bytes 2097152 | tf_op jit(solution)/shard_map/top_k | solution.py:30
  16.0 1.2 copy.26
  17.3 0.7 reshape.380
  18.0 6.0 %all-to-all-start = ((f32[8,1,1024]{2,1,0:T(1,128)}), f32[8,1,1024]{2,1,0:T(1,128)S(1)}, u32[]{:S(2)}, u32[]{:S(2)}) async-start(f32[8,1,1024]{2,1,0:T(1,128)} %reshape.380), calls=%async_computation | async-start | bytes 65536 | tf_op jit(solution)/shard_map/all_to_all | solution.py:31
  24.0 4.5 all-to-all-done
  28.5 0.6 broadcast.326
  29.1 0.8 reduce.13
  29.9 0.1 reshape.381
  30.0 0.1 copy.19
  30.1 0.1 reshape.267
  30.1 2.6 sort_prefixfusion
  32.7 0.7 multiply_reduce_fusion.1
  33.5 0.7 and_reduce_fusion.1
  34.3 4.3 scatter_custom_fusion.2
  38.7 0.1 reshape.268
  38.8 0.7 reshape.382
  39.5 4.0 all-to-all-start.1
  43.5 0.2 copy.27
  43.8 0.1 reshape.270
  43.9 4.2 all-to-all-done.1
  48.1 0.8 reduce.14
  48.9 0.1 reshape.383
  49.0 0.1 convert_element_type.49
  49.1 2.3 reduce-window.14
  51.4 0.3 slice_reduce_fusion.1
  51.7 0.2 reduce-window.15
  51.8 0.1 add_add_fusion
  51.9 0.1 gt.14
  52.1 0.1 multiply_reduce_fusion
  52.2 0.1 and_reduce_fusion
  52.3 30.4 %scatter_custom_fusion.3 = s32[2048]{0:T(1024)S(1)} fusion(s32[8192]{0:T(1024)S(1)} %get-tuple-element.24, s32[8192]{0:T(1024)S(1)} %get-tuple-element.23, s32[]{:T(128)} %constant.107.clone.1), kind=kCustom, calls=%fused_computation.111 | custom fusion | bytes 8196
  82.8 13.0 %gather_fusion.4 = s32[2048]{0:T(1024)S(1)} fusion(s32[8,1024]{1,0:T(8,128)S(1)} %reshape.270, s32[2048]{0:T(1024)S(1)} %bitcast.66), kind=kCustom, calls=%fused_computation.4 | custom fusion | bytes 32768 | tf_op jit(solution)/shard_map/jit(take_along_axis)/gather | solution.py:46
  95.8 0.1 compare_select_fusion.6
  95.9 18.2 %gather_fusion.1 = bf16[2048,2048]{1,0:T(8,128)(2,1)} fusion(bf16[512,2048]{1,0:T(8,128)(2,1)} %param.6, s32[2048]{0:T(1024)S(1)} %broadcast_clamp_fusion), kind=kCustom, calls=%fused_computation.1 | custom fusion | bytes 16785408 | tf_op jit(solution)/shard_map/jit(_take)/gather | solution.py:47
  114.1 7.4 %broadcast_select_fusion = bf16[8,256,2048]{2,1,0:T(8,128)(2,1)} fusion(bf16[8,256,2048]{2,1,0:T(8,128)(2,1)} %bitcast.69, pred[8,256]{1,0:T(8,128)(4,1)S(1)} %compare_and_fusion.1), kind=kLoop, calls=%fused_computation.11 | loop fusion | flops 4194304 | bytes 16779264 | tf_op jit(solution)/shard_map/jit(_take)/select_n | solution.py:47
  121.6 5.6 %all-to-all-start.2 = ((bf16[8,256,2048]{2,1,0:T(8,128)(2,1)}), bf16[8,256,2048]{2,1,0:T(8,128)(2,1)}, u32[]{:S(2)}, u32[]{:S(2)}) async-start(bf16[8,256,2048]{2,1,0:T(8,128)(2,1)} %broadcast_select_fusion), calls=%async_computation.2 | async-start | bytes 16777216 | tf_op jit(solution)/shard_map/all_to_all | solution.py:48
  127.2 0.1 reshape.273
  127.3 2.3 reduce-window.16
  129.6 0.1 reshape.274
  129.6 0.3 slice_reduce_fusion
  129.9 0.2 reduce-window.19
  130.2 0.1 fusion.35
  130.3 0.1 reshape.277
  130.5 8.6 %gather_fusion.5 = s32[1024]{0:T(1024)S(1)} fusion(s32[32,256]{1,0:T(8,128)S(1)} %reshape.277, s32[1024]{0:T(1024)S(1)} %reshape.329), kind=kCustom, calls=%fused_computation.5 | custom fusion | bytes 16384 | tf_op jit(solution)/shard_map/jit(take_along_axis)/gather | solution.py:39
  139.2 0.1 reshape.278
  139.3 4.3 scatter_custom_fusion
  143.6 77.1 %all-to-all-done.2 = bf16[8,256,2048]{2,1,0:T(8,128)(2,1)} async-done(((bf16[8,256,2048]{2,1,0:T(8,128)(2,1)}), bf16[8,256,2048]{2,1,0:T(8,128)(2,1)}, u32[]{:S(2)}, u32[]{:S(2)}) %all-to-all-start.2) | async-done | bytes 8388640 | tf_op jit(solution)/shard_map/all_to_all | solution.py:48
  220.8 13.3 %gather_fusion.2 = bf16[1024,2048]{1,0:T(8,128)(2,1)} fusion(bf16[2048,2048]{1,0:T(8,128)(2,1)} %bitcast.11, s32[1024]{0:T(1024)S(1)} %broadcast_clamp_fusion.2), kind=kCustom, calls=%fused_computation.2 | custom fusion | bytes 8392704 | tf_op jit(solution)/shard_map/jit(_take)/gather | solution.py:49
  234.0 24.6 %fusion.10.clone.4 = bf16[32,32,512]{2,1,0:T(8,128)(2,1)S(1)} fusion(bf16[32,2048,512]{2,1,0:T(8,128)(2,1)} %param.8, bf16[32,32,2048]{2,1,0:T(8,128)(2,1)} %bitcast.70, pred[32,32]{1,0:T(8,128)(4,1)S(1)} %get-tuple-element.18), kind=kOutput, calls=%fused_computation.27.clone.clone.clone.1 | convolution fusion | flops 2154299392 | bytes 72352768 | tf_op jit(solution)/shard_map/ecd,edf->ecf/dot_general | solution.py:10
  258.7 25.6 %convolution_convert_fusion = bf16[32,32,2048]{2,1,0:T(8,128)(2,1)} fusion(bf16[32,512,2048]{2,1,0:T(8,128)(2,1)} %param.9, bf16[32,32,512]{2,1,0:T(8,128)(2,1)S(1)} %fusion.10.clone.4), kind=kOutput, calls=%fused_computation.17 | convolution fusion | flops 2149580800 | bytes 72351744 | tf_op jit(solution)/shard_map/ecf,efd->ecd/dot_general | solution.py:11
  284.3 19.0 %gather_fusion.3 = bf16[2048,2048]{1,0:T(8,128)(2,1)} fusion(bf16[1024,2048]{1,0:T(8,128)(2,1)} %bitcast.64, s32[2048]{0:T(1024)S(1)} %fusion.48), kind=kCustom, calls=%fused_computation.3 | custom fusion | bytes 16785408 | tf_op jit(solution)/shard_map/jit(_take)/gather | solution.py:52
  303.4 7.4 %broadcast_select_fusion.1 = bf16[8,256,2048]{2,1,0:T(8,128)(2,1)} fusion(bf16[8,256,2048]{2,1,0:T(8,128)(2,1)} %bitcast.68, pred[8,256]{1,0:T(8,128)(4,1)S(1)} %broadcast_in_dim.110), kind=kLoop, calls=%fused_computation.12 | loop fusion | flops 4194304 | bytes 16779264 | tf_op jit(solution)/shard_map/jit(_take)/select_n | solution.py:52
  310.8 6.1 %all-to-all-start.3 = ((bf16[8,256,2048]{2,1,0:T(8,128)(2,1)}), bf16[8,256,2048]{2,1,0:T(8,128)(2,1)}, u32[]{:S(2)}, u32[]{:S(2)}) async-start(bf16[8,256,2048]{2,1,0:T(8,128)(2,1)} %broadcast_select_fusion.1), calls=%async_computation.3 | async-start | bytes 16777216 | tf_op jit(solution)/shard_map/all_to_all | solution.py:53
  316.9 0.1 reduce_max.9
  317.0 0.2 fusion.33
  317.3 0.2 divide_bitcast_fusion
  317.5 0.3 copy.33
  317.8 7.4 %convert_add_fusion = f32[512,2048]{1,0:T(8,128)} fusion(bf16[512,2048]{1,0:T(8,128)(2,1)} %param.6, bf16[512,2048]{1,0:T(8,128)(2,1)S(1)} %copy-done, bf16[2048,512]{1,0:T(8,128)(2,1)} %param.10), kind=kOutput, calls=%fused_computation.15 | convolution fusion | flops 2154037248 | bytes 10485760 | tf_op jit(solution)/shard_map/dot_general | solution.py:16
  325.2 11.8 %gather_fusion = f32[2048]{0:T(1024)S(1)} fusion(f32[131072]{0:T(1024)S(1)} %bitcast.65, s32[2048]{0:T(1024)S(1)} %broadcast_clamp_fusion.1), kind=kCustom, calls=%fused_computation | custom fusion | bytes 24576 | tf_op jit(solution)/shard_map/jit(_take)/gather | solution.py:56
  337.0 0.2 convert_reduce_fusion
  337.3 73.2 %all-to-all-done.3 = bf16[8,256,2048]{2,1,0:T(8,128)(2,1)} async-done(((bf16[8,256,2048]{2,1,0:T(8,128)(2,1)}), bf16[8,256,2048]{2,1,0:T(8,128)(2,1)}, u32[]{:S(2)}, u32[]{:S(2)}) %all-to-all-start.3) | async-done | bytes 8388640 | tf_op jit(solution)/shard_map/all_to_all | solution.py:53
  410.5 10.3 %convert_multiply_fusion = f32[8,256,2048]{2,1,0:T(8,128)} fusion(bf16[8,256,2048]{2,1,0:T(8,128)(2,1)} %all-to-all-done.3, f32[8,256]{1,0:T(8,128)S(1)} %select_select_fusion), kind=kLoop, calls=%fused_computation.10 | loop fusion | flops 8388608 | bytes 25174016 | tf_op jit(solution)/shard_map/mul | solution.py:57
  420.7 31.4 %scatter_fusion = f32[512,2048]{1,0:T(8,128)} fusion(f32[512,2048]{1,0:T(8,128)} %convert_add_fusion, s32[2048]{0:T(1024)S(1)} %bitcast.77, f32[2048,2048]{1,0:T(8,128)} %bitcast.67), kind=kCustom, calls=%fused_computation.7 | custom fusion | flops 4194304 | bytes 50339840 | tf_op jit(solution)/shard_map/scatter-add | solution.py:58
  452.1 3.8 convert_element_type.53
  (55 shorter events, 0.8 us)
Async XLA Ops:
  0.0 317.8 %copy-start = (bf16[512,2048]{1,0:T(8,128)(2,1)S(1)}, bf16[512,2048]{1,0:T(8,128)(2,1)}, u32[]{:S(2)}) copy-start(bf16[512,2048]{1,0:T(8,128)(2,1)} %param.11) | copy-start | bytes 6291460
  0.0 52.1 %copy-start.3 = (s32[2]{0:T(128)S(1)}, s32[2]{0:T(128)}, u32[]{:S(2)}) copy-start(s32[2]{0:T(128)} %constant.166) | copy-start | bytes 28
  0.0 52.2 %copy-start.4 = (s32[2]{0:T(128)S(1)}, s32[2]{0:T(128)}, u32[]{:S(2)}) copy-start(s32[2]{0:T(128)} %constant.175) | copy-start | bytes 28
  18.0 10.5 %all-to-all-start = ((f32[8,1,1024]{2,1,0:T(1,128)}), f32[8,1,1024]{2,1,0:T(1,128)S(1)}, u32[]{:S(2)}, u32[]{:S(2)}) async-start(f32[8,1,1024]{2,1,0:T(1,128)} %reshape.380), calls=%async_computation | async-start | bytes 65536 | tf_op jit(solution)/shard_map/all_to_all | solution.py:31
  39.5 8.6 %all-to-all-start.1 = ((f32[8,1,1024]{2,1,0:T(1,128)}), f32[8,1,1024]{2,1,0:T(1,128)S(1)}, u32[]{:S(2)}, u32[]{:S(2)}) async-start(f32[8,1,1024]{2,1,0:T(1,128)} %reshape.382), calls=%async_computation.1 | async-start | bytes 65536 | tf_op jit(solution)/shard_map/all_to_all | solution.py:40
  121.6 99.2 %all-to-all-start.2 = ((bf16[8,256,2048]{2,1,0:T(8,128)(2,1)}), bf16[8,256,2048]{2,1,0:T(8,128)(2,1)}, u32[]{:S(2)}, u32[]{:S(2)}) async-start(bf16[8,256,2048]{2,1,0:T(8,128)(2,1)} %broadcast_select_fusion), calls=%async_computation.2 | async-start | bytes 16777216 | tf_op jit(solution)/shard_map/all_to_all | solution.py:48
  310.8 6.1 %copy-start.2 = (f32[512,256]{1,0:T(8,128)S(1)}, f32[512,256]{1,0:T(8,128)}, u32[]{:S(2)}) copy-start(f32[512,256]{1,0:T(8,128)} %param.7) | copy-start | bytes 1572868
  310.8 99.7 %all-to-all-start.3 = ((bf16[8,256,2048]{2,1,0:T(8,128)(2,1)}), bf16[8,256,2048]{2,1,0:T(8,128)(2,1)}, u32[]{:S(2)}, u32[]{:S(2)}) async-start(bf16[8,256,2048]{2,1,0:T(8,128)(2,1)} %broadcast_select_fusion.1), calls=%async_computation.3 | async-start | bytes 16777216 | tf_op jit(solution)/shard_map/all_to_all | solution.py:53
  420.7 35.2 %copy-start.1 = (bf16[512,2048]{1,0:T(8,128)(2,1)S(1)}, bf16[512,2048]{1,0:T(8,128)(2,1)}, u32[]{:S(2)}) copy-start(bf16[512,2048]{1,0:T(8,128)(2,1)} %param.11) | copy-start | bytes 6291460
where the time goes:
time: 457 us; the launch traced here: 456 us
  waiting for transfers between devices  159 us (35%)
  local copies, waits for them, and re-layouts  129 us (28%)
  other arithmetic  88.2 us (19%)
  matrix products  57.6 us (13%)
  starting transfers between devices  21.6 us (5%)
    all_to_all x1, waiting for transfers between devices, local_layer(): recv_rows = lax.all_to_all(send_rows, 'ep', 0, 0)  77.1 us
    all_to_all x1, waiting for transfers between devices, local_layer(): returned = lax.all_to_all(back_rows, 'ep', 0, 0)  73.2 us
    unnamed x24, local copies, waits for them, and re-layouts  36.8 us
    scatter-add x1, other arithmetic, local_layer(): jax.ops.segment_sum(weighted, slot_tok.reshape(-1), num_segments=tok_loc)  31.4 us
    dot_general x1, matrix products, expert_ffn(): jnp.einsum('ecf,efd->ecd', hidden, w_out, preferred_element_type=jnp.floa...  25.6 us
    dot_general x1, matrix products, expert_ffn(): jnp.einsum('ecd,edf->ecf', expert_rows, w_in, preferred_element_type=jnp....  24.6 us
    gather x1, local copies, waits for them, and re-layouts, local_layer(): jnp.take(expert_out.reshape(num_local * capacity, d_model), back_index, a...  19 us
    gather x1, local copies, waits for them, and re-layouts, local_layer(): jnp.take(x_rows, slot_tok.reshape(-1), axis=0)  18.2 us
  transfers between devices with their start and end apart: 4, of which 4 were waited for; matrix products, arithmetic and copies ran while one was open for 8% of the time, Pallas kernels for 0%

commit v1 on v0

v1 whole, which is shorter than its diff:
```python
import functools

import jax
import jax.numpy as jnp
from jax import lax
from jax.experimental import pallas as pl
from jax.experimental.pallas import tpu as pltpu
from jax.sharding import PartitionSpec as P

CAP_FACTOR = 2
MESH = pl.DeviceIdType.MESH
F32 = jnp.float32
BF16 = jnp.bfloat16
VMEM_BYTES = 64 * 1024 * 1024 - 65536
EXPERT_GROUP = 4


def dot(a, b):
    return jnp.dot(a, b, preferred_element_type=F32)


def gelu(v):
    return jax.nn.gelu(v)


def entry_barrier(me, n):
    barrier = pltpu.get_barrier_semaphore()
    for i in range(1, n):
        pl.semaphore_signal(barrier, inc=1, device_id={"ep": lax.rem(me + i, n)}, device_id_type=MESH)
    pl.semaphore_wait(barrier, n - 1)


def dispatch_kernel(n, chunks, x_hbm, lt_ref, w_hbm, ws_ref, h_ref, hs_ref, route_ref,
                    xb, ltr, scores, probs, pick, xg, hacc, wbuf,
                    x_sem, lt_loc, lt_ss, lt_rs, ss, rs, w_sem):
    me = lax.axis_index("ep")
    core = lax.rem(me, 2)
    partner = me + 1 - 2 * core
    right, left = lax.rem(me + 2, n), lax.rem(me + n - 2, n)
    far = lax.rem(me + 4, n)
    tok_loc, d_model = x_hbm.shape
    num_local, _, ff = w_hbm.shape
    tokens = n * tok_loc
    dc = d_model // chunks
    half = tok_loc // 2
    cap = h_ref.shape[0] // num_local
    groups = num_local // EXPERT_GROUP
    steps = chunks * groups
    depth = wbuf.shape[0]

    def w_copy(step):
        c, g = step // groups, lax.rem(step, groups)
        slot = lax.rem(step, depth)
        return pltpu.make_async_copy(w_hbm.at[pl.ds(g * EXPERT_GROUP, EXPERT_GROUP), pl.ds(c * dc, dc), :], wbuf.at[slot], w_sem.at[slot])

    x_copies = [pltpu.make_async_copy(x_hbm.at[:, pl.ds(c * dc, dc)], xb.at[c, me], x_sem.at[c]) for c in range(chunks)]
    for cp in x_copies:
        cp.start()
    lt_own = pltpu.make_async_copy(lt_ref.at[me], ltr.at[me], lt_loc.at[0])
    lt_own.start()
    for step in range(depth - 1):
        w_copy(step).start()

    entry_barrier(me, n)

    lt_copies = []
    for i in range(1, n):
        dst = lax.rem(me + i, n)
        cp = pltpu.make_async_remote_copy(src_ref=lt_ref.at[dst], dst_ref=ltr.at[me], send_sem=lt_ss.at[i], recv_sem=lt_rs.at[i], device_id={"ep": dst}, device_id_type=MESH)
        cp.start()
        lt_copies.append(cp)

    sent = []

    def send(c, kind, block, rows, to):
        ref = xb.at[c, block] if rows is None else xb.at[c, block, pl.ds(rows, half)]
        cp = pltpu.make_async_remote_copy(src_ref=ref, dst_ref=ref, send_sem=ss.at[c, kind], recv_sem=rs.at[c, kind], device_id={"ep": to}, device_id_type=MESH)
        cp.start()
        sent.append(cp)

    def landed(c, kind, block, rows=None):
        ref = xb.at[c, block] if rows is None else xb.at[c, block, pl.ds(rows, half)]
        pltpu.make_async_remote_copy(src_ref=ref, dst_ref=ref, send_sem=ss.at[c, kind], recv_sem=rs.at[c, kind], device_id={"ep": partner}, device_id_type=MESH).wait_recv()

    def send_own(c):
        x_copies[c].wait()
        send(c, 0, me, None, right)
        send(c, 1, me, None, left)
        send(c, 2, me, None, partner)

    def forward_near(c):
        landed(c, 0, left)
        send(c, 5, left, 0, right)
        send(c, 3, left, None, partner)
        landed(c, 1, right)
        send(c, 6, right, half, left)
        send(c, 4, right, None, partner)

    def forward_far(c):
        landed(c, 5, far, 0)
        send(c, 7, far, 0, partner)
        landed(c, 6, far, half)
        send(c, 8, far, half, partner)

    def flip(d):
        return d + 1 - 2 * core

    def land_partner(c):
        landed(c, 2, partner)
        landed(c, 3, flip(left))
        landed(c, 4, flip(right))
        landed(c, 7, flip(far), 0)
        landed(c, 8, flip(far), half)

    send_own(0)
    if chunks > 1:
        send_own(1)

    @pl.loop(0, tok_loc // 128)
    def _(t):
        rows = pl.ds(pl.multiple_of(t * 128, 128), 128)
        acc = dot(xb[0, me, rows, :], ws_ref[pl.ds(0, dc), :])
        hs_ref[rows, :] = acc

    lt_own.wait()
    for cp in lt_copies:
        cp.wait()
    for s in range(n):
        cols = pl.ds(s * tok_loc, tok_loc)
        block = ltr[s, 0:num_local, :]
        scores[:, cols] = block
        probs[:, cols] = jnp.exp(block - ltr[s, num_local:num_local + 1, :]) / ltr[s, num_local + 1:num_local + 2, :]

    per_row = 128 // cap
    lane = lax.broadcasted_iota(jnp.int32, (num_local, 128), 1)
    home = lax.rem(lax.broadcasted_iota(jnp.int32, (num_local, 128), 0), per_row) * cap
    tok_iota = lax.broadcasted_iota(jnp.int32, (num_local, tokens), 1).astype(F32)

    def extract(j, carry):
        tok_tab, gate_tab = carry
        cur = scores[...]
        top = jnp.max(cur, axis=1, keepdims=True)
        hit = cur == top
        tok = jnp.sum(jnp.where(hit, tok_iota, 0.0), axis=1, keepdims=True)
        gate = jnp.sum(jnp.where(hit, probs[...], 0.0), axis=1, keepdims=True)
        scores[...] = jnp.where(hit, -jnp.inf, cur)
        here = lane == home + j
        return jnp.where(here, tok, tok_tab), jnp.where(here, gate, gate_tab)

    zero = jnp.zeros((num_local, 128), F32)
    tok_tab, gate_tab = lax.fori_loop(0, cap, extract, (zero, zero))
    nrow = num_local // per_row
    tok_rows = [jnp.sum(tok_tab[g * per_row:(g + 1) * per_row], axis=0, keepdims=True) for g in range(nrow)]
    gate_rows = [jnp.sum(gate_tab[g * per_row:(g + 1) * per_row], axis=0, keepdims=True) for g in range(nrow)]
    tok_flat = jnp.concatenate(tok_rows, axis=1)
    gate_flat = jnp.concatenate(gate_rows, axis=1)

    tok_cols = jnp.concatenate(tok_rows, axis=0).T
    for g in range(nrow):
        col = tok_cols[:, g:g + 1]

        @pl.loop(0, n)
        def _(s):
            ids = lax.broadcasted_iota(jnp.int32, (128, tok_loc), 1).astype(F32) + (s * tok_loc).astype(F32)
            pick[pl.ds(g * 128, 128), pl.ds(pl.multiple_of(s * tok_loc, tok_loc), tok_loc)] = jnp.where(ids == col, 1.0, 0.0).astype(BF16)

    rows_total = num_local * cap
    src = jnp.floor(tok_flat * (1.0 / tok_loc))
    loc = tok_flat - src * tok_loc
    of_src = jnp.where(lax.broadcasted_iota(jnp.int32, (n, rows_total), 0).astype(F32) == src, 1.0, 0.0)
    before = jnp.where(lax.broadcasted_iota(jnp.int32, (rows_total, rows_total), 0) < lax.broadcasted_iota(jnp.int32, (rows_total, rows_total), 1), 1.0, 0.0).astype(BF16)
    count = dot(of_src.astype(BF16), before)
    slot = jnp.sum(of_src * count, axis=0, keepdims=True)
    pair_cap = 2 * tok_loc * CAP_FACTOR // n
    hi = jnp.floor(loc * (1.0 / 16))
    g_hi = gate_flat.astype(BF16).astype(F32)
    g_mid = (gate_flat - g_hi).astype(BF16).astype(F32)
    g_lo = gate_flat - g_hi - g_mid
    route_ref[0:1, :] = hi
    route_ref[1:2, :] = loc - 16 * hi
    route_ref[2:3, :] = jnp.ones_like(hi)
    route_ref[3:4, :] = g_hi
    route_ref[4:5, :] = g_mid
    route_ref[5:6, :] = g_lo
    route_ref[6:7, :] = src * pair_cap + slot
    route_ref[7:8, :] = jnp.zeros_like(hi)

    def compute(c):
        @pl.loop(0, rows_total // 256)
        def _(t):
            rows = pl.ds(pl.multiple_of(t * 256, 256), 256)
            acc = dot(pick[rows, 0:tok_loc], xb[c, 0])
            for s in range(1, n):
                acc += dot(pick[rows, s * tok_loc:(s + 1) * tok_loc], xb[c, s])
            xg[rows, :] = acc.astype(BF16)

        @pl.loop(0, groups)
        def _(g):
            step = c * groups + g

            @pl.when(step + depth - 1 < steps)
            def _():
                w_copy(step + depth - 1).start()

            w_copy(step).wait()
            buf = lax.rem(step, depth)
            for i in range(EXPERT_GROUP):
                rows = pl.ds(pl.multiple_of((g * EXPERT_GROUP + i) * cap, cap), cap)
                part = dot(xg[rows, :], wbuf[buf, i])
                hacc[rows, :] = part if c == 0 else hacc[rows, :] + part

    for c in range(chunks):
        forward_near(c)
        if c + 2 < chunks:
            send_own(c + 2)
        if c > 0:
            forward_far(c - 1)
            land_partner(c - 1)
            compute(c - 1)
            @pl.loop(0, tok_loc // 128)
            def _(t):
                rows = pl.ds(pl.multiple_of(t * 128, 128), 128)
                hs_ref[rows, :] += dot(xb[c, me, rows, :], ws_ref[pl.ds(c * dc, dc), :])
    forward_far(chunks - 1)
    land_partner(chunks - 1)
    compute(chunks - 1)

    @pl.loop(0, rows_total // 128)
    def _(t):
        rows = pl.ds(pl.multiple_of(t * 128, 128), 128)
        h_ref[rows, :] = gelu(hacc[rows, :]).astype(BF16)

    for cp in sent:
        cp.wait_send()


def combine_kernel(n, chunks, h_ref, route_ref, w_hbm, x_ref, hs_ref, ws_ref, out_ref,
                   sel, z, sendb, recvb, metas, metar, cmat, hsb, wbuf,
                   m_ss, m_rs, ss, rs, w_sem):
    me = lax.axis_index("ep")
    tok_loc, d_model = x_ref.shape
    num_local, ff, _ = w_hbm.shape
    rows_total = h_ref.shape[0]
    cap = rows_total // num_local
    slots = sel.shape[0]
    pair_cap = slots // n
    dc = d_model // chunks
    groups = num_local // EXPERT_GROUP
    steps = chunks * groups
    depth = wbuf.shape[0]

    def w_copy(step):
        c, g = step // groups, lax.rem(step, groups)
        slot = lax.rem(step, depth)
        return pltpu.make_async_copy(w_hbm.at[pl.ds(g * EXPERT_GROUP, EXPERT_GROUP), :, pl.ds(pl.multiple_of(c * dc, dc), dc)], wbuf.at[slot], w_sem.at[slot])

    for step in range(depth - 1):
        w_copy(step).start()
    entry_barrier(me, n)

    for g in range(rows_total // 128):
        key = route_ref[6:7, g * 128:(g + 1) * 128]

        @pl.loop(0, slots // 256)
        def _(t):
            ids = lax.broadcasted_iota(jnp.int32, (256, 128), 0).astype(F32) + (t * 256).astype(F32)
            sel[pl.ds(pl.multiple_of(t * 256, 256), 256), pl.ds(g * 128, 128)] = jnp.where(ids == key, 1.0, 0.0).astype(BF16)

    vals = route_ref[...].astype(BF16)

    @pl.loop(0, n)
    def _(d):
        block = sel[pl.ds(pl.multiple_of(d * pair_cap, pair_cap), pair_cap), :]
        metas[d] = lax.dot_general(vals, block, (((1,), (1,)), ((), ())), preferred_element_type=F32)

    metar[me] = metas[me]
    meta_copies = []
    for i in range(1, n):
        dst = lax.rem(me + i, n)
        cp = pltpu.make_async_remote_copy(src_ref=metas.at[dst], dst_ref=metar.at[me], send_sem=m_ss.at[i], recv_sem=m_rs.at[i], device_id={"ep": dst}, device_id_type=MESH)
        cp.start()
        meta_copies.append(cp)

    def produce(c):
        @pl.loop(0, groups)
        def _(g):
            step = c * groups + g

            @pl.when(step + depth - 1 < steps)
            def _():
                w_copy(step + depth - 1).start()

            w_copy(step).wait()
            buf = lax.rem(step, depth)
            for i in range(EXPERT_GROUP):
                rows = pl.ds(pl.multiple_of((g * EXPERT_GROUP + i) * cap, cap), cap)
                z[rows, :] = dot(h_ref[rows, :], wbuf[buf, i]).astype(BF16)

        copies = []
        for i in list(range(1, n)) + [0]:
            dst = lax.rem(me + i, n)
            rows = pl.ds(pl.multiple_of(dst * pair_cap, pair_cap), pair_cap)
            mine = pl.ds(pl.multiple_of(me * pair_cap, pair_cap), pair_cap)
            block = dot(sel[rows, :], z[...]).astype(BF16)
            if i == 0:
                recvb[c, mine, :] = block
            else:
                sendb[c, rows, :] = block
                cp = pltpu.make_async_remote_copy(src_ref=sendb.at[c, rows], dst_ref=recvb.at[c, mine], send_sem=ss.at[c, i], recv_sem=rs.at[c, i], device_id={"ep": dst}, device_id_type=MESH)
                cp.start()
                copies.append(cp)
        return copies

    def build_weights():
        for cp in meta_copies:
            cp.wait()

        @pl.loop(0, n)
        def _(o):
            hi, lo, valid = metar[o, 0:1, :], metar[o, 1:2, :], metar[o, 2:3, :]
            tok = 16.0 * hi + lo + valid - 1.0
            ids = lax.broadcasted_iota(jnp.int32, (tok_loc, pair_cap), 0).astype(F32)
            hit = ids == tok
            for k in range(3):
                part = jnp.where(hit, metar[o, 3 + k:4 + k, :], 0.0).astype(BF16)
                cmat[k, :, pl.ds(pl.multiple_of(o * pair_cap, pair_cap), pair_cap)] = part

        hsb[...] = gelu(hs_ref[...]).astype(BF16)

    def finish(c, copies):
        for cp in copies:
            cp.wait()

        @pl.loop(0, tok_loc // 128)
        def _(t):
            rows = pl.ds(pl.multiple_of(t * 128, 128), 128)
            acc = dot(cmat[0, rows, :], recvb[c])
            acc += dot(cmat[1, rows, :], recvb[c])
            acc += dot(cmat[2, rows, :], recvb[c])
            cols = slice(c * dc, (c + 1) * dc)
            shared = dot(hsb[rows, :], ws_ref[:, cols]).astype(BF16).astype(F32)
            out_ref[rows, cols] = (x_ref[rows, cols].astype(F32) + (acc + shared)).astype(BF16)

    pending = produce(0)
    build_weights()
    for c in range(1, chunks):
        nxt = produce(c)
        finish(c - 1, pending)
        pending = nxt
    finish(chunks - 1, pending)


def solution(mesh):
    n = mesh.shape["ep"]
    chunks_a, chunks_b, depth = 4, 4, 4

    def local_layer(x_rows, logits, w_in, w_out, shared_in, shared_out):
        tok_loc, d_model = x_rows.shape
        experts = logits.shape[1]
        num_local = experts // n
        cap = tok_loc * n * CAP_FACTOR // experts
        pair_cap = 2 * tok_loc * CAP_FACTOR // n
        ff = w_in.shape[2]
        tokens, rows_total, slots = n * tok_loc, num_local * cap, n * pair_cap
        dca, dcb = d_model // chunks_a, d_model // chunks_b

        top = jnp.max(logits, axis=1)
        total = jnp.sum(jnp.exp(logits - top[:, None]), axis=1)
        stats = jnp.stack([top, total] + [jnp.zeros_like(top)] * 6)
        lt = jnp.concatenate([logits.T.reshape(n, num_local, tok_loc), jnp.broadcast_to(stats, (n, 8, tok_loc))], axis=1)

        vmem = pl.BlockSpec(memory_space=pltpu.VMEM)
        hbm = pl.BlockSpec(memory_space=pl.ANY)
        dma = pltpu.SemaphoreType.DMA
        h, hs, route = pl.pallas_call(
            functools.partial(dispatch_kernel, n, chunks_a),
            out_shape=[jax.ShapeDtypeStruct((rows_total, ff), BF16), jax.ShapeDtypeStruct((tok_loc, ff), F32), jax.ShapeDtypeStruct((8, rows_total), F32)],
            in_specs=[hbm, vmem, hbm, vmem],
            out_specs=[vmem, vmem, vmem],
            scratch_shapes=[
                pltpu.VMEM((chunks_a, n, tok_loc, dca), BF16),
                pltpu.VMEM((n, num_local + 8, tok_loc), F32),
                pltpu.VMEM((num_local, tokens), F32),
                pltpu.VMEM((num_local, tokens), F32),
                pltpu.VMEM((rows_total, tokens), BF16),
                pltpu.VMEM((rows_total, dca), BF16),
                pltpu.VMEM((rows_total, ff), F32),
                pltpu.VMEM((depth, EXPERT_GROUP, dca, ff), BF16),
                dma((chunks_a,)), dma((1,)), dma((n,)), dma((n,)),
                dma((chunks_a, 9)), dma((chunks_a, 9)), dma((depth,)),
            ],
            compiler_params=pltpu.CompilerParams(collective_id=0, has_side_effects=True, vmem_limit_bytes=VMEM_BYTES),
            name="dispatch",
        )(x_rows, lt, w_in, shared_in)

        return pl.pallas_call(
            functools.partial(combine_kernel, n, chunks_b),
            out_shape=jax.ShapeDtypeStruct((tok_loc, d_model), BF16),
            in_specs=[vmem, vmem, hbm, vmem, vmem, vmem],
            out_specs=vmem,
            scratch_shapes=[
                pltpu.VMEM((slots, rows_total), BF16),
                pltpu.VMEM((rows_total, dcb), BF16),
                pltpu.VMEM((chunks_b, slots, dcb), BF16),
                pltpu.VMEM((chunks_b, slots, dcb), BF16),
                pltpu.VMEM((n, 8, pair_cap), F32),
                pltpu.VMEM((n, 8, pair_cap), F32),
                pltpu.VMEM((3, tok_loc, slots), BF16),
                pltpu.VMEM((tok_loc, shared_in.shape[1]), BF16),
                pltpu.VMEM((depth, EXPERT_GROUP, ff, dcb), BF16),
                dma((n,)), dma((n,)), dma((chunks_b, n)), dma((chunks_b, n)), dma((depth,)),
            ],
            compiler_params=pltpu.CompilerParams(collective_id=1, has_side_effects=True, vmem_limit_bytes=VMEM_BYTES),
            name="combine",
        )(h, route, w_out, x_rows, hs, shared_out)

    row_spec = P(("dp", "ep"), None)
    expert_spec = P("ep", None, None)
    return jax.shard_map(local_layer, mesh=mesh, in_specs=(row_spec, row_spec, expert_spec, expert_spec, P(None, None), P(None, None)), out_specs=row_spec, check_vma=False)
```

time: 457 us -> 225 us (0.49)
  Pallas kernels: 0 us -> 217 us
  waiting for transfers between devices: 159 us -> 0 us
  local copies, waits for them, and re-layouts: 129 us -> 4.57 us
  other arithmetic: 88.2 us -> 3.43 us
  matrix products: 57.6 us -> 0 us
  starting transfers between devices: 21.6 us -> 0 us
    pallas_call x0 -> x2, Pallas kernels: none -> 217 us  [the longest x1 114 us: local_layer(): pl.pallas_call(functools.partial(combine_kernel, n, chunks_b), out_shape=...]
    all_to_all x4 -> x0, waiting for transfers between devices: 159 us -> none  [the longest x1 77.1 us: local_layer(): recv_rows = lax.all_to_all(send_rows, 'ep', 0, 0)]
    gather x9 -> x0, local copies, waits for them, and re-layouts: 84 us -> none  [the longest x1 19 us: local_layer(): jnp.take(expert_out.reshape(num_local * capacity, d_model), back_index, a...]
    dot_general x3 -> x0, matrix products: 57.6 us -> none  [the longest x1 25.6 us: expert_ffn(): jnp.einsum('ecf,efd->ecd', hidden, w_out, preferred_element_type=jnp.floa...]
    unnamed x24 -> x1, local copies, waits for them, and re-layouts: 36.8 us -> 3.16 us
    scatter-add x1 -> x0, other arithmetic: 31.4 us -> none  [local_layer(): jax.ops.segment_sum(weighted, slot_tok.reshape(-1), num_segments=tok_loc)]
    all_to_all x4 -> x0, starting transfers between devices: 21.6 us -> none  [the longest x1 6.06 us: local_layer(): returned = lax.all_to_all(back_rows, 'ep', 0, 0)]
    top_k x2 -> x0, other arithmetic: 18.5 us -> none  [the longest x1 15.9 us: local_layer(): cand_score, cand_tok = lax.top_k(logits.T, cand_len)]
  transfers between devices with their start and end apart: 4 -> 0, of which waited for: 4 -> 0; matrix products, arithmetic and copies ran while one was open for 8% -> 0% of each run, Pallas kernels for 0% -> 0%
where the time goes in v1:
time: 225 us
  Pallas kernels  217 us (96%)
  local copies, waits for them, and re-layouts  4.57 us (2%)
  other arithmetic  3.43 us (2%)
    pallas_call x1, Pallas kernels, local_layer(): pl.pallas_call(functools.partial(combine_kernel, n, chunks_b), out_shape=...  114 us
    pallas_call x1, Pallas kernels, local_layer(): pl.pallas_call(functools.partial(dispatch_kernel, n, chunks_a), out_shape...  103 us

profile of v1, /device:TPU:113, one launch (start us, length us, event | category | flops | bytes accessed | tf_op | source)
XLA Modules:
  0.0 224.9 jit_solution(639926757404251856)
XLA Ops:
  0.0 0.1 pad.4.clone
  0.1 0.1 pad.5.clone
  0.2 1.2 reduce_max.9
  1.3 1.3 exponential_reduce_fusion
  2.6 0.1 maximum_maximum_fusion
  2.7 1.2 copy.7
  4.0 0.9 pad_maximum_fusion.lt_ref
  4.9 103.2 %dispatch.1 = (bf16[1024,512]{1,0:T(8,128)(2,1)}, f32[512,512]{1,0:T(8,128)}, f32[8,1024]{1,0:T(8,128)}) custom-call(bf16[512,2048]{1,0:T(8,128)(2,1)} %x_ref.1, f32[8,40,512]{2,1,0:T(8,128)} %pad_maximum_fusion.lt_ref, bf16[32,2048,512]{2,1,0:T(8,128)(2,1)} %w_hbm.2, bf16[2048,512]{1,0:T(8,128)(2,1)} %ws_ref.2), custom_call_target="tpu_custom_call" | custom-call | tf_op jit(solution)/shard_map/dispatch/pallas_call | solution.py:375
  108.1 113.6 %combine.1 = bf16[512,2048]{1,0:T(8,128)(2,1)} custom-call(bf16[1024,512]{1,0:T(8,128)(2,1)} %get-tuple-element.8.h_ref, f32[8,1024]{1,0:T(8,128)} %get-tuple-element.9.route_ref, bf16[32,512,2048]{2,1,0:T(8,128)(2,1)} %w_hbm.3, bf16[512,2048]{1,0:T(8,128)(2,1)} %x_ref.1, f32[512,512]{1,0:T(8,128)} %get-tuple-element.10.hs_ref, bf16[512,2048]{1,0:T(8,128)(2,1)} %ws_ref.3), custom_call_target="tpu_custom_call" | custom-call | tf_op jit(solution)/shard_map/combine/pallas_call | solution.py:396
  221.7 3.2 %copy.9 = bf16[512,2048]{1,0:T(8,128)(2,1)} copy(bf16[512,2048]{1,0:T(8,128)(2,1)} %combine.1) | data formatting | bytes 4194304
  (3 shorter events, 0.0 us)

commit v2 on v0

v2 whole, which is shorter than its diff:
```python
import functools

import jax
import jax.numpy as jnp
from jax import lax
from jax.experimental import pallas as pl
from jax.experimental.pallas import tpu as pltpu
from jax.sharding import PartitionSpec as P

CAP_FACTOR = 2
MESH = pl.DeviceIdType.MESH
F32 = jnp.float32
BF16 = jnp.bfloat16
VMEM_BYTES = 64 * 1024 * 1024 - 65536
EXPERT_GROUP = 4
UNIT = 256
SEND_SLOTS = 3
W1_DEPTH = 4
W2_DEPTH = 8
KINDS = 9


def dot(a, b):
    return jnp.dot(a, b, preferred_element_type=F32)


def gelu(v):
    return jax.nn.gelu(v)


def tile(i, size):
    return pl.ds(pl.multiple_of(i * size, size), size)


def layer_kernel(n, x_hbm, lg_hbm, w1_hbm, ws1_hbm, w2_hbm, ws2_hbm, out_hbm,
                 xb, pick, sel, sendb, recvb, xg, hacc, w1buf, w2buf, z, h, hsb, ws1, ws2, stage,
                 sc, gate_p, cand, cand_t, cand_r, m_sc, m_tok, m_gate, route, metas, metar,
                 x_sem, in_sem, c_ss, c_rs, ss, rs, w1_sem, w2_sem, m_ss, m_rs, a_ss, a_rs, o_sem):
    me = lax.axis_index("ep")
    core = lax.rem(me, 2)
    partner = me + 1 - 2 * core
    right, left = lax.rem(me + 2, n), lax.rem(me + n - 2, n)
    far = lax.rem(me + 4, n)
    tok_loc, d_model = x_hbm.shape
    num_local, _, ff = w1_hbm.shape
    nu = d_model // UNIT
    half = tok_loc // 2
    rows_total = hacc.shape[0]
    cap = rows_total // num_local
    slots = sel.shape[0]
    pair_cap = slots // n
    groups = num_local // EXPERT_GROUP
    steps = nu * groups

    def flip(d):
        return d + 1 - 2 * core

    def w1_copy(step):
        u, g, slot = step // groups, lax.rem(step, groups), lax.rem(step, W1_DEPTH)
        return pltpu.make_async_copy(w1_hbm.at[tile(g, EXPERT_GROUP), tile(u, UNIT), :], w1buf.at[slot], w1_sem.at[slot])

    def w2_copy(step):
        u, g, slot = step // groups, lax.rem(step, groups), lax.rem(step, W2_DEPTH)
        return pltpu.make_async_copy(w2_hbm.at[tile(g, EXPERT_GROUP), :, tile(u, UNIT)], w2buf.at[slot], w2_sem.at[slot])

    own = tile(me, tok_loc)
    x_copies = [pltpu.make_async_copy(x_hbm.at[:, pl.ds(u * UNIT, UNIT)], xb.at[u, own], x_sem.at[u]) for u in range(nu)]
    lg_copy = pltpu.make_async_copy(lg_hbm, sc, in_sem.at[0])
    ws1_copy = pltpu.make_async_copy(ws1_hbm, ws1, in_sem.at[1])
    ws2_copy = pltpu.make_async_copy(ws2_hbm, ws2, in_sem.at[2])
    for cp in x_copies + [lg_copy, ws1_copy]:
        cp.start()
    barrier = pltpu.get_barrier_semaphore()
    for i in range(1, n):
        pl.semaphore_signal(barrier, inc=1, device_id={"ep": lax.rem(me + i, n)}, device_id_type=MESH)
    for step in range(W1_DEPTH - 1):
        w1_copy(step).start()
    for cp in x_copies:
        cp.wait()
    pl.semaphore_wait(barrier, n - 1)

    def hop(u, kind, block, part, to):
        rows = tile(block, tok_loc) if part is None else tile(2 * block + part, half)
        ref = xb.at[u, rows]
        return pltpu.make_async_remote_copy(src_ref=ref, dst_ref=ref, send_sem=ss.at[u, kind], recv_sem=rs.at[u, kind], device_id={"ep": to}, device_id_type=MESH)

    def send_own(u):
        hop(u, 0, me, None, right).start()
        hop(u, 1, me, None, left).start()
        hop(u, 2, me, None, partner).start()

    def forward_near(u):
        hop(u, 0, left, None, partner).wait_recv()
        hop(u, 5, left, 0, right).start()
        hop(u, 3, left, None, partner).start()
        hop(u, 1, right, None, partner).wait_recv()
        hop(u, 6, right, 1, left).start()
        hop(u, 4, right, None, partner).start()

    def forward_far(u):
        hop(u, 5, far, 0, partner).wait_recv()
        hop(u, 7, far, 0, partner).start()
        hop(u, 6, far, 1, partner).wait_recv()
        hop(u, 8, far, 1, partner).start()

    def land_partner(u):
        hop(u, 2, partner, None, partner).wait_recv()
        hop(u, 3, flip(left), None, partner).wait_recv()
        hop(u, 4, flip(right), None, partner).wait_recv()
        hop(u, 7, flip(far), 0, partner).wait_recv()
        hop(u, 8, flip(far), 1, partner).wait_recv()

    send_own(0)
    send_own(1)

    lg_copy.wait()
    ws2_copy.start()
    raw = sc[...]
    ex = jnp.exp(raw - jnp.max(raw, axis=1, keepdims=True))
    gate_p[...] = ex / jnp.sum(ex, axis=1, keepdims=True)
    cand[...] = jnp.zeros_like(cand)
    tok_iota = lax.broadcasted_iota(jnp.int32, sc.shape, 0).astype(F32)

    @pl.loop(0, cap)
    def _(j):
        cur = sc[...]
        top = jnp.max(cur, axis=0, keepdims=True)
        hit = cur == top
        cand[pl.ds(j, 1), :] = top
        cand[pl.ds(cap + j, 1), :] = jnp.sum(jnp.where(hit, tok_iota, 0.0), axis=0, keepdims=True)
        cand[pl.ds(2 * cap + j, 1), :] = jnp.sum(jnp.where(hit, gate_p[...], 0.0), axis=0, keepdims=True)
        sc[...] = jnp.where(hit, -jnp.inf, cur)

    flat_t = cand[...].T
    for d in range(n):
        cand_t[d] = flat_t[d * num_local:(d + 1) * num_local]
    cand_r[me] = cand_t[me]
    cand_copies = []
    for i in range(1, n):
        dst = lax.rem(me + i, n)
        cp = pltpu.make_async_remote_copy(src_ref=cand_t.at[dst], dst_ref=cand_r.at[me], send_sem=c_ss.at[i], recv_sem=c_rs.at[i], device_id={"ep": dst}, device_id_type=MESH)
        cp.start()
        cand_copies.append(cp)

    forward_near(0)
    send_own(2)

    ws1_copy.wait()

    @pl.loop(0, tok_loc // 128)
    def _(t):
        rows = pl.ds(pl.multiple_of(me * tok_loc + t * 128, 128), 128)
        acc = dot(xb[0, rows, :], ws1[0:UNIT, :])
        for u in range(1, nu):
            acc += dot(xb[u, rows, :], ws1[u * UNIT:(u + 1) * UNIT, :])
        hsb[tile(t, 128), :] = gelu(acc).astype(BF16)

    forward_near(1)
    send_own(3)

    for cp in cand_copies:
        cp.wait()
    lane = lax.broadcasted_iota(jnp.int32, (num_local, 128), 1)
    for s in range(n):
        block = cand_r[s]
        m_sc[s] = jnp.where(lane < cap, block, -jnp.inf)
        m_tok[s] = pltpu.roll(block, 128 - cap, 1) + float(s) * tok_loc
        m_gate[s] = pltpu.roll(block, 128 - 2 * cap, 1)

    per_row = 128 // cap
    home = lax.rem(lax.broadcasted_iota(jnp.int32, (num_local, 128), 0), per_row) * cap

    def extract(j, carry):
        tok_tab, gate_tab = carry
        cur = m_sc[...]
        top = jnp.max(jnp.max(cur, axis=0), axis=1, keepdims=True)
        hit = cur == top[None]
        tok = jnp.sum(jnp.sum(jnp.where(hit, m_tok[...], 0.0), axis=0), axis=1, keepdims=True)
        gate = jnp.sum(jnp.sum(jnp.where(hit, m_gate[...], 0.0), axis=0), axis=1, keepdims=True)
        m_sc[...] = jnp.where(hit, -jnp.inf, cur)
        here = lane == home + j
        return jnp.where(here, tok, tok_tab), jnp.where(here, gate, gate_tab)

    zero = jnp.zeros((num_local, 128), F32)
    tok_tab, gate_tab = lax.fori_loop(0, cap, extract, (zero, zero))
    nrow = num_local // per_row
    tok_rows = [jnp.sum(tok_tab[g * per_row:(g + 1) * per_row], axis=0, keepdims=True) for g in range(nrow)]
    gate_rows = [jnp.sum(gate_tab[g * per_row:(g + 1) * per_row], axis=0, keepdims=True) for g in range(nrow)]
    tok_flat = jnp.concatenate(tok_rows, axis=1)
    gate_flat = jnp.concatenate(gate_rows, axis=1)

    tok_cols = jnp.concatenate(tok_rows, axis=0).T
    for g in range(nrow):
        col = tok_cols[:, g:g + 1]

        @pl.loop(0, n)
        def _(s):
            ids = lax.broadcasted_iota(jnp.int32, (128, tok_loc), 1).astype(F32) + (s * tok_loc).astype(F32)
            pick[pl.ds(g * 128, 128), tile(s, tok_loc)] = jnp.where(ids == col, 1.0, 0.0).astype(BF16)

    source = jnp.floor(tok_flat * (1.0 / tok_loc))
    loc = tok_flat - source * tok_loc
    of_src = jnp.where(lax.broadcasted_iota(jnp.int32, (n, rows_total), 0).astype(F32) == source, 1.0, 0.0)
    sq = (rows_total, rows_total)
    before = jnp.where(lax.broadcasted_iota(jnp.int32, sq, 0) < lax.broadcasted_iota(jnp.int32, sq, 1), 1.0, 0.0).astype(BF16)
    slot = jnp.sum(of_src * dot(of_src.astype(BF16), before), axis=0, keepdims=True)
    hi = jnp.floor(loc * (1.0 / 16))
    g_hi = gate_flat.astype(BF16).astype(F32)
    g_mid = (gate_flat - g_hi).astype(BF16).astype(F32)
    route[0:1, :] = hi
    route[1:2, :] = loc - 16 * hi
    route[2:3, :] = jnp.ones_like(hi)
    route[3:4, :] = g_hi
    route[4:5, :] = g_mid
    route[5:6, :] = gate_flat - g_hi - g_mid
    route[6:7, :] = source * pair_cap + slot
    route[7:8, :] = jnp.zeros_like(hi)

    def meta_copy(i):
        dst = lax.rem(me + i, n)
        return pltpu.make_async_remote_copy(src_ref=metas.at[dst], dst_ref=metar.at[me], send_sem=m_ss.at[i], recv_sem=m_rs.at[i], device_id={"ep": dst}, device_id_type=MESH)

    def announce():
        for g in range(rows_total // 128):
            key = route[6:7, g * 128:(g + 1) * 128]

            @pl.loop(0, slots // 256)
            def _(t):
                ids = lax.broadcasted_iota(jnp.int32, (256, 128), 0).astype(F32) + (t * 256).astype(F32)
                sel[tile(t, 256), pl.ds(g * 128, 128)] = jnp.where(ids == key, 1.0, 0.0).astype(BF16)

        vals = route[...].astype(BF16)

        @pl.loop(0, n)
        def _(d):
            metas[d] = lax.dot_general(vals, sel[tile(d, pair_cap), :], (((1,), (1,)), ((), ())), preferred_element_type=F32)

        metar[me] = metas[me]
        for i in range(1, n):
            meta_copy(i).start()

    hacc[...] = jnp.zeros_like(hacc)

    def gather(u):
        @pl.loop(0, rows_total // 256)
        def _(t):
            xg[tile(t, 256), :] = dot(pick[tile(t, 256), :], xb[u]).astype(BF16)

    def first_product(u):
        @pl.loop(0, groups)
        def _(g):
            step = u * groups + g

            @pl.when(step + W1_DEPTH - 1 < steps)
            def _():
                w1_copy(step + W1_DEPTH - 1).start()

            w1_copy(step).wait()
            buf = lax.rem(step, W1_DEPTH)
            for i in range(EXPERT_GROUP):
                rows = tile(g * EXPERT_GROUP + i, cap)
                hacc[rows, :] += dot(xg[rows, :], w1buf[buf, i])

    forward_far(0)

    @pl.loop(2, nu + 2)
    def _(u):
        @pl.when(u < nu)
        def _():
            forward_near(u)

        @pl.when(u + 2 < nu)
        def _():
            send_own(u + 2)

        @pl.when(u == 4)
        def _():
            announce()

        land_partner(u - 2)
        gather(u - 2)

        @pl.when(u - 1 < nu)
        def _():
            forward_far(u - 1)

        @pl.when(u == nu)
        def _():
            for step in range(W2_DEPTH - 1):
                w2_copy(step).start()

        first_product(u - 2)

    @pl.loop(0, rows_total // 128)
    def _(t):
        h[tile(t, 128), :] = gelu(hacc[tile(t, 128), :]).astype(BF16)

    def back(u, i):
        dst = lax.rem(me + i, n)
        return pltpu.make_async_remote_copy(src_ref=sendb.at[lax.rem(u, SEND_SLOTS), tile(dst, pair_cap)], dst_ref=recvb.at[u, tile(me, pair_cap)], send_sem=a_ss.at[u, i], recv_sem=a_rs.at[u, i], device_id={"ep": dst}, device_id_type=MESH)

    def produce(u):
        @pl.loop(0, groups)
        def _(g):
            step = u * groups + g

            @pl.when(step + W2_DEPTH - 1 < steps)
            def _():
                w2_copy(step + W2_DEPTH - 1).start()

            w2_copy(step).wait()
            buf = lax.rem(step, W2_DEPTH)
            for i in range(EXPERT_GROUP):
                rows = tile(g * EXPERT_GROUP + i, cap)
                z[rows, :] = dot(h[rows, :], w2buf[buf, i]).astype(BF16)

        @pl.when(u >= SEND_SLOTS)
        def _():
            for i in range(1, n):
                back(u - SEND_SLOTS, i).wait_send()

        @pl.loop(1, n)
        def _(i):
            rows = tile(lax.rem(me + i, n), pair_cap)
            sendb[lax.rem(u, SEND_SLOTS), rows, :] = dot(sel[rows, :], z[...]).astype(BF16)
            back(u, i).start()

        recvb[u, tile(me, pair_cap), :] = dot(sel[tile(me, pair_cap), :], z[...]).astype(BF16)

    def weights_at(k):
        return (tok_loc if k == 1 else 0), (slots if k == 2 else 0)

    def build_weights():
        for i in range(1, n):
            meta_copy(i).wait()

        @pl.loop(0, n)
        def _(o):
            tok = 16.0 * metar[o, 0:1, :] + metar[o, 1:2, :] + metar[o, 2:3, :] - 1.0
            hit = lax.broadcasted_iota(jnp.int32, (tok_loc, pair_cap), 0).astype(F32) == tok
            for k in range(3):
                r0, c0 = weights_at(k)
                pick[pl.ds(r0, tok_loc), pl.ds(pl.multiple_of(c0 + o * pair_cap, pair_cap), pair_cap)] = jnp.where(hit, metar[o, 3 + k:4 + k, :], 0.0).astype(BF16)

    def out_copy(u):
        return pltpu.make_async_copy(stage.at[lax.rem(u, 2)], out_hbm.at[:, tile(u, UNIT)], o_sem.at[lax.rem(u, 2)])

    def finish(u):
        for i in range(1, n):
            back(u, i).wait_recv()

        @pl.when(u >= 2)
        def _():
            out_copy(u - 2).wait()

        @pl.loop(0, tok_loc // 128)
        def _(t):
            acc = jnp.zeros((128, UNIT), F32)
            for k in range(3):
                r0, c0 = weights_at(k)
                acc += dot(pick[pl.ds(pl.multiple_of(r0 + t * 128, 128), 128), c0:c0 + slots], recvb[u])
            shared = dot(hsb[tile(t, 128), :], ws2[:, tile(u, UNIT)]).astype(BF16).astype(F32)
            x_own = xb[u, pl.ds(pl.multiple_of(me * tok_loc + t * 128, 128), 128), :].astype(F32)
            stage[lax.rem(u, 2), tile(t, 128), :] = (x_own + (acc + shared)).astype(BF16)

        out_copy(u).start()

    produce(0)
    build_weights()
    ws2_copy.wait()

    @pl.loop(1, nu)
    def _(u):
        produce(u)
        finish(u - 1)

    finish(nu - 1)
    out_copy(nu - 2).wait()
    out_copy(nu - 1).wait()

    @pl.loop(nu - SEND_SLOTS, nu)
    def _(u):
        for i in range(1, n):
            back(u, i).wait_send()

    @pl.loop(0, nu)
    def _(u):
        hop(u, 0, me, None, right).wait_send()
        hop(u, 1, me, None, left).wait_send()
        hop(u, 2, me, None, partner).wait_send()
        hop(u, 3, left, None, partner).wait_send()
        hop(u, 4, right, None, partner).wait_send()
        hop(u, 5, left, 0, right).wait_send()
        hop(u, 6, right, 1, left).wait_send()
        hop(u, 7, far, 0, partner).wait_send()
        hop(u, 8, far, 1, partner).wait_send()


def solution(mesh):
    n = mesh.shape["ep"]

    def local_layer(x_rows, logits, w_in, w_out, shared_in, shared_out):
        tok_loc, d_model = x_rows.shape
        experts = logits.shape[1]
        num_local = experts // n
        cap = tok_loc * n * CAP_FACTOR // experts
        pair_cap = 2 * tok_loc * CAP_FACTOR // n
        ff = w_in.shape[2]
        tokens, rows_total, slots = n * tok_loc, num_local * cap, n * pair_cap
        nu = d_model // UNIT
        hbm = pl.BlockSpec(memory_space=pl.ANY)
        dma = pltpu.SemaphoreType.DMA
        vmem = pltpu.VMEM
        return pl.pallas_call(
            functools.partial(layer_kernel, n),
            out_shape=jax.ShapeDtypeStruct((tok_loc, d_model), BF16),
            in_specs=[hbm] * 6,
            out_specs=hbm,
            scratch_shapes=[
                vmem((nu, tokens, UNIT), BF16),
                vmem((rows_total, tokens), BF16),
                vmem((slots, rows_total), BF16),
                vmem((SEND_SLOTS, slots, UNIT), BF16),
                vmem((nu, slots, UNIT), BF16),
                vmem((rows_total, UNIT), BF16),
                vmem((rows_total, ff), F32),
                vmem((W1_DEPTH, EXPERT_GROUP, UNIT, ff), BF16),
                vmem((W2_DEPTH, EXPERT_GROUP, ff, UNIT), BF16),
                vmem((rows_total, UNIT), BF16),
                vmem((rows_total, ff), BF16),
                vmem((tok_loc, shared_in.shape[1]), BF16),
                vmem(shared_in.shape, BF16),
                vmem(shared_out.shape, BF16),
                vmem((2, tok_loc, UNIT), BF16),
                vmem((tok_loc, experts), F32),
                vmem((tok_loc, experts), F32),
                vmem((128, experts), F32),
                vmem((n, num_local, 128), F32),
                vmem((n, num_local, 128), F32),
                vmem((n, num_local, 128), F32),
                vmem((n, num_local, 128), F32),
                vmem((n, num_local, 128), F32),
                vmem((8, rows_total), F32),
                vmem((n, 8, pair_cap), F32),
                vmem((n, 8, pair_cap), F32),
                dma((nu,)), dma((3,)), dma((n,)), dma((n,)), dma((nu, KINDS)), dma((nu, KINDS)),
                dma((W1_DEPTH,)), dma((W2_DEPTH,)), dma((n,)), dma((n,)), dma((nu, n)), dma((nu, n)), dma((2,)),
            ],
            compiler_params=pltpu.CompilerParams(collective_id=0, has_side_effects=True, vmem_limit_bytes=VMEM_BYTES),
            name="moe_layer",
        )(x_rows, logits, w_in, shared_in, w_out, shared_out)

    row_spec = P(("dp", "ep"), None)
    expert_spec = P("ep", None, None)
    return jax.shard_map(local_layer, mesh=mesh, in_specs=(row_spec, row_spec, expert_spec, expert_spec, P(None, None), P(None, None)), out_specs=row_spec, check_vma=False)
```

time: 457 us -> 196 us (0.43)
  Pallas kernels: 0 us -> 193 us
  waiting for transfers between devices: 159 us -> 0 us
  local copies, waits for them, and re-layouts: 129 us -> 3.16 us
  other arithmetic: 88.2 us -> 0 us
  matrix products: 57.6 us -> 0 us
  starting transfers between devices: 21.6 us -> 0 us
    pallas_call x0 -> x1, Pallas kernels: none -> 193 us  [local_layer(): pl.pallas_call(functools.partial(layer_kernel, n), out_shape=jax.ShapeDty...]
    all_to_all x4 -> x0, waiting for transfers between devices: 159 us -> none  [the longest x1 77.1 us: local_layer(): recv_rows = lax.all_to_all(send_rows, 'ep', 0, 0)]
    gather x9 -> x0, local copies, waits for them, and re-layouts: 84 us -> none  [the longest x1 19 us: local_layer(): jnp.take(expert_out.reshape(num_local * capacity, d_model), back_index, a...]
    dot_general x3 -> x0, matrix products: 57.6 us -> none  [the longest x1 25.6 us: expert_ffn(): jnp.einsum('ecf,efd->ecd', hidden, w_out, preferred_element_type=jnp.floa...]
    unnamed x24 -> x1, local copies, waits for them, and re-layouts: 36.8 us -> 3.16 us
    scatter-add x1 -> x0, other arithmetic: 31.4 us -> none  [local_layer(): jax.ops.segment_sum(weighted, slot_tok.reshape(-1), num_segments=tok_loc)]
    all_to_all x4 -> x0, starting transfers between devices: 21.6 us -> none  [the longest x1 6.06 us: local_layer(): returned = lax.all_to_all(back_rows, 'ep', 0, 0)]
    top_k x2 -> x0, other arithmetic: 18.5 us -> none  [the longest x1 15.9 us: local_layer(): cand_score, cand_tok = lax.top_k(logits.T, cand_len)]
  transfers between devices with their start and end apart: 4 -> 0, of which waited for: 4 -> 0; matrix products, arithmetic and copies ran while one was open for 8% -> 0% of each run, Pallas kernels for 0% -> 0%
where the time goes in v2:
time: 196 us
  Pallas kernels  193 us (98%)
  local copies, waits for them, and re-layouts  3.16 us (2%)
    pallas_call x1, Pallas kernels, local_layer(): pl.pallas_call(functools.partial(layer_kernel, n), out_shape=jax.ShapeDty...  193 us

profile of v2, /device:TPU:113, one launch (start us, length us, event | category | flops | bytes accessed | tf_op | source)
XLA Modules:
  0.0 196.1 jit_solution(10254962306074498961)
XLA Ops:
  0.0 192.9 %moe_layer.1 = bf16[512,2048]{1,0:T(8,128)(2,1)} custom-call(bf16[512,2048]{1,0:T(8,128)(2,1)} %x_hbm.1, f32[512,256]{1,0:T(8,128)} %lg_hbm.1, bf16[32,2048,512]{2,1,0:T(8,128)(2,1)} %w1_hbm.1, bf16[2048,512]{1,0:T(8,128)(2,1)} %ws1_hbm.1, bf16[32,512,2048]{2,1,0:T(8,128)(2,1)} %w2_hbm.1, bf16[512,2048]{1,0:T(8,128)(2,1)} %ws2_hbm.1), custom_call_target="tpu_custom_call" | custom-call | tf_op jit(solution)/shard_map/moe_layer/pallas_call | solution.py:414
  192.9 3.2 %copy.8 = bf16[512,2048]{1,0:T(8,128)(2,1)} copy(bf16[512,2048]{1,0:T(8,128)(2,1)} %moe_layer.1) | data formatting | bytes 4194304

commit v3 on v2

--- a/solution.py
+++ b/solution.py
@@ -15,7 +15,7 @@
 EXPERT_GROUP = 4
 UNIT = 256
 SEND_SLOTS = 3
-W1_DEPTH = 4
+W1_DEPTH = 6
 W2_DEPTH = 8
 KINDS = 9
 
@@ -33,9 +33,9 @@
 
 
 def layer_kernel(n, x_hbm, lg_hbm, w1_hbm, ws1_hbm, w2_hbm, ws2_hbm, out_hbm,
-                 xb, pick, sel, sendb, recvb, xg, hacc, w1buf, w2buf, z, h, hsb, ws1, ws2, stage,
+                 xb, pick, sel, sendb, xg, hacc, w1buf, w2buf, z, h, hsb, ws1, ws2, stage,
                  sc, gate_p, cand, cand_t, cand_r, m_sc, m_tok, m_gate, route, metas, metar,
-                 x_sem, in_sem, c_ss, c_rs, ss, rs, w1_sem, w2_sem, m_ss, m_rs, a_ss, a_rs, o_sem):
+                 x_sem, in_sem, c_ss, c_rs, ss, rs, w1_sem, w2_sem, m_ss, m_rs, a_ss, a_rs, o_sem, free_sem):
     me = lax.axis_index("ep")
     core = lax.rem(me, 2)
     partner = me + 1 - 2 * core
@@ -75,6 +75,8 @@
         pl.semaphore_signal(barrier, inc=1, device_id={"ep": lax.rem(me + i, n)}, device_id_type=MESH)
     for step in range(W1_DEPTH - 1):
         w1_copy(step).start()
+    for step in range(W2_DEPTH - 1):
+        w2_copy(step).start()
     for cp in x_copies:
         cp.wait()
     pl.semaphore_wait(barrier, n - 1)
@@ -103,10 +105,12 @@
         hop(u, 6, far, 1, partner).wait_recv()
         hop(u, 8, far, 1, partner).start()
 
-    def land_partner(u):
+    def land_near(u):
         hop(u, 2, partner, None, partner).wait_recv()
         hop(u, 3, flip(left), None, partner).wait_recv()
         hop(u, 4, flip(right), None, partner).wait_recv()
+
+    def land_far(u):
         hop(u, 7, flip(far), 0, partner).wait_recv()
         hop(u, 8, flip(far), 1, partner).wait_recv()
 
@@ -240,34 +244,66 @@
             meta_copy(i).start()
 
     hacc[...] = jnp.zeros_like(hacc)
-
-    def gather(u):
+    chip = 2 * tok_loc
+    near_chips = [lax.rem(me // 2 + k, n // 2) for k in (0, 1, n // 2 - 1)]
+    far_chip = far // 2
+
+    def gather_near(u):
+        land_near(u)
+
         @pl.loop(0, rows_total // 256)
         def _(t):
-            xg[tile(t, 256), :] = dot(pick[tile(t, 256), :], xb[u]).astype(BF16)
-
-    def first_product(u):
-        @pl.loop(0, groups)
+            acc = dot(pick[tile(t, 256), tile(near_chips[0], chip)], xb[u, tile(near_chips[0], chip), :])
+            for q in near_chips[1:]:
+                acc += dot(pick[tile(t, 256), tile(q, chip)], xb[u, tile(q, chip), :])
+            xg[lax.rem(u, 2), tile(t, 256), :] = acc.astype(BF16)
+
+    def gather_far(u):
+        land_far(u)
+
+        @pl.loop(0, rows_total // 256)
+        def _(t):
+            acc = dot(pick[tile(t, 256), tile(far_chip, chip)], xb[u, tile(far_chip, chip), :])
+            xg[lax.rem(u, 2), tile(t, 256), :] = (xg[lax.rem(u, 2), tile(t, 256), :].astype(F32) + acc).astype(BF16)
+
+    def next_w1(step):
+        @pl.when(step + W1_DEPTH - 1 < steps)
+        def _():
+            w1_copy(step + W1_DEPTH - 1).start()
+
+        w1_copy(step).wait()
+        return lax.rem(step, W1_DEPTH)
+
+    def next_w2(step):
+        @pl.when(step + W2_DEPTH - 1 < steps)
+        def _():
+            w2_copy(step + W2_DEPTH - 1).start()
+
+        w2_copy(step).wait()
+        return lax.rem(step, W2_DEPTH)
+
+    def first_product(u, lo, hi_):
+        @pl.loop(lo, hi_)
         def _(g):
-            step = u * groups + g
-
-            @pl.when(step + W1_DEPTH - 1 < steps)
-            def _():
-                w1_copy(step + W1_DEPTH - 1).start()
-
-            w1_copy(step).wait()
-            buf = lax.rem(step, W1_DEPTH)
+            buf = next_w1(u * groups + g)
             for i in range(EXPERT_GROUP):
                 rows = tile(g * EXPERT_GROUP + i, cap)
-                hacc[rows, :] += dot(xg[rows, :], w1buf[buf, i])
+                hacc[rows, :] += dot(xg[lax.rem(u, 2), rows, :], w1buf[buf, i])
 
     forward_far(0)
 
-    @pl.loop(2, nu + 2)
+    @pl.loop(2, 4)
     def _(u):
-        @pl.when(u < nu)
-        def _():
-            forward_near(u)
+        forward_near(u)
+        send_own(u + 2)
+        gather_near(u - 2)
+        gather_far(u - 2)
+        forward_far(u - 1)
+        first_product(u - 2, 0, groups)
+
+    @pl.loop(4, nu)
+    def _(u):
+        forward_near(u)
 
         @pl.when(u + 2 < nu)
         def _():
@@ -275,113 +311,24 @@
 
         @pl.when(u == 4)
         def _():
+            gather_near(2)
+            gather_far(2)
+            first_product(2, 0, groups)
             announce()
-
-        land_partner(u - 2)
-        gather(u - 2)
-
-        @pl.when(u - 1 < nu)
-        def _():
-            forward_far(u - 1)
-
-        @pl.when(u == nu)
-        def _():
-            for step in range(W2_DEPTH - 1):
-                w2_copy(step).start()
-
-        first_product(u - 2)
-
-    @pl.loop(0, rows_total // 128)
-    def _(t):
-        h[tile(t, 128), :] = gelu(hacc[tile(t, 128), :]).astype(BF16)
-
-    def back(u, i):
-        dst = lax.rem(me + i, n)
-        return pltpu.make_async_remote_copy(src_ref=sendb.at[lax.rem(u, SEND_SLOTS), tile(dst, pair_cap)], dst_ref=recvb.at[u, tile(me, pair_cap)], send_sem=a_ss.at[u, i], recv_sem=a_rs.at[u, i], device_id={"ep": dst}, device_id_type=MESH)
-
-    def produce(u):
-        @pl.loop(0, groups)
-        def _(g):
-            step = u * groups + g
-
-            @pl.when(step + W2_DEPTH - 1 < steps)
-            def _():
-                w2_copy(step + W2_DEPTH - 1).start()
-
-            w2_copy(step).wait()
-            buf = lax.rem(step, W2_DEPTH)
-            for i in range(EXPERT_GROUP):
-                rows = tile(g * EXPERT_GROUP + i, cap)
-                z[rows, :] = dot(h[rows, :], w2buf[buf, i]).astype(BF16)
-
-        @pl.when(u >= SEND_SLOTS)
-        def _():
-            for i in range(1, n):
-                back(u - SEND_SLOTS, i).wait_send()
-
-        @pl.loop(1, n)
-        def _(i):
-            rows = tile(lax.rem(me + i, n), pair_cap)
-            sendb[lax.rem(u, SEND_SLOTS), rows, :] = dot(sel[rows, :], z[...]).astype(BF16)
-            back(u, i).start()
-
-        recvb[u, tile(me, pair_cap), :] = dot(sel[tile(me, pair_cap), :], z[...]).astype(BF16)
-
-    def weights_at(k):
-        return (tok_loc if k == 1 else 0), (slots if k == 2 else 0)
-
-    def build_weights():
-        for i in range(1, n):
-            meta_copy(i).wait()
-
-        @pl.loop(0, n)
-        def _(o):
-            tok = 16.0 * metar[o, 0:1, :] + metar[o, 1:2, :] + metar[o, 2:3, :] - 1.0
-            hit = lax.broadcasted_iota(jnp.int32, (tok_loc, pair_cap), 0).astype(F32) == tok
-            for k in range(3):
-                r0, c0 = weights_at(k)
-                pick[pl.ds(r0, tok_loc), pl.ds(pl.multiple_of(c0 + o * pair_cap, pair_cap), pair_cap)] = jnp.where(hit, metar[o, 3 + k:4 + k, :], 0.0).astype(BF16)
-
-    def out_copy(u):
-        return pltpu.make_async_copy(stage.at[lax.rem(u, 2)], out_hbm.at[:, tile(u, UNIT)], o_sem.at[lax.rem(u, 2)])
-
-    def finish(u):
-        for i in range(1, n):
-            back(u, i).wait_recv()
-
-        @pl.when(u >= 2)
-        def _():
-            out_copy(u - 2).wait()
-
-        @pl.loop(0, tok_loc // 128)
-        def _(t):
-            acc = jnp.zeros((128, UNIT), F32)
-            for k in range(3):
-                r0, c0 = weights_at(k)
-                acc += dot(pick[pl.ds(pl.multiple_of(r0 + t * 128, 128), 128), c0:c0 + slots], recvb[u])
-            shared = dot(hsb[tile(t, 128), :], ws2[:, tile(u, UNIT)]).astype(BF16).astype(F32)
-            x_own = xb[u, pl.ds(pl.multiple_of(me * tok_loc + t * 128, 128), 128), :].astype(F32)
-            stage[lax.rem(u, 2), tile(t, 128), :] = (x_own + (acc + shared)).astype(BF16)
-
-        out_copy(u).start()
-
-    produce(0)
-    build_weights()
-    ws2_copy.wait()
-
-    @pl.loop(1, nu)
-    def _(u):
-        produce(u)
-        finish(u - 1)
-
-    finish(nu - 1)
-    out_copy(nu - 2).wait()
-    out_copy(nu - 1).wait()
-
-    @pl.loop(nu - SEND_SLOTS, nu)
-    def _(u):
-        for i in range(1, n):
-            back(u, i).wait_send()
+            gather_near(3)
+
+        gather_near(u)
+        forward_far(u - 1)
+        gather_far(u - 1)
+        first_product(u - 1, 0, groups // 2)
+
+        @pl.when(u == nu - 1)
+        def _():
+            forward_far(nu - 1)
+
+        first_product(u - 1, groups // 2, groups)
+
+    gather_far(nu - 1)
 
     @pl.loop(0, nu)
     def _(u):
@@ -394,6 +341,120 @@
         hop(u, 6, right, 1, left).wait_send()
         hop(u, 7, far, 0, partner).wait_send()
         hop(u, 8, far, 1, partner).wait_send()
+
+    for i in range(1, n):
+        pl.semaphore_signal(free_sem, inc=1, device_id={"ep": lax.rem(me + i, n)}, device_id_type=MESH)
+
+    @pl.loop(0, groups)
+    def _(g):
+        buf1, buf2 = next_w1((nu - 1) * groups + g), next_w2(g)
+        for i in range(EXPERT_GROUP):
+            rows = tile(g * EXPERT_GROUP + i, cap)
+            act = gelu(hacc[rows, :] + dot(xg[(nu - 1) % 2, rows, :], w1buf[buf1, i])).astype(BF16)
+            h[rows, :] = act
+            z[rows, :] = dot(act, w2buf[buf2, i]).astype(BF16)
+
+    pl.semaphore_wait(free_sem, n - 1)
+
+    def landing(d):
+        return (n // 2) * tok_loc * (1 - d // (n // 2))
+
+    def back(u, i):
+        dst = lax.rem(me + i, n)
+        return pltpu.make_async_remote_copy(src_ref=sendb.at[lax.rem(u, SEND_SLOTS), tile(dst, pair_cap)], dst_ref=xb.at[u, pl.ds(pl.multiple_of(landing(dst) + me * pair_cap, pair_cap), pair_cap)], send_sem=a_ss.at[u, i], recv_sem=a_rs.at[u, i], device_id={"ep": dst}, device_id_type=MESH)
+
+    def arrived(u, i):
+        src = lax.rem(me + n - i, n)
+        ref = xb.at[u, pl.ds(pl.multiple_of(landing(me) + src * pair_cap, pair_cap), pair_cap)]
+        pltpu.make_async_remote_copy(src_ref=ref, dst_ref=ref, send_sem=a_ss.at[u, i], recv_sem=a_rs.at[u, i], device_id={"ep": partner}, device_id_type=MESH).wait_recv()
+
+    def second_product(u):
+        @pl.loop(0, groups)
+        def _(g):
+            buf = next_w2(u * groups + g)
+            for i in range(EXPERT_GROUP):
+                rows = tile(g * EXPERT_GROUP + i, cap)
+                z[rows, :] = dot(h[rows, :], w2buf[buf, i]).astype(BF16)
+
+    def send_back(u):
+        @pl.when(u >= SEND_SLOTS)
+        def _():
+            for i in range(1, n):
+                back(u - SEND_SLOTS, i).wait_send()
+
+        @pl.loop(1, n)
+        def _(i):
+            rows = tile(lax.rem(me + i, n), pair_cap)
+            sendb[lax.rem(u, SEND_SLOTS), rows, :] = dot(sel[rows, :], z[...]).astype(BF16)
+            back(u, i).start()
+
+        xb[u, pl.ds(pl.multiple_of(landing(me) + me * pair_cap, pair_cap), pair_cap), :] = dot(sel[tile(me, pair_cap), :], z[...]).astype(BF16)
+
+    def weights_at(k):
+        return (tok_loc if k == 1 else 0), (slots if k == 2 else 0)
+
+    def build_weights():
+        for i in range(1, n):
+            meta_copy(i).wait()
+
+        @pl.loop(0, n)
+        def _(o):
+            tok = 16.0 * metar[o, 0:1, :] + metar[o, 1:2, :] + metar[o, 2:3, :] - 1.0
+            hit = lax.broadcasted_iota(jnp.int32, (tok_loc, pair_cap), 0).astype(F32) == tok
+            for k in range(3):
+                r0, c0 = weights_at(k)
+                pick[pl.ds(r0, tok_loc), pl.ds(pl.multiple_of(c0 + o * pair_cap, pair_cap), pair_cap)] = jnp.where(hit, metar[o, 3 + k:4 + k, :], 0.0).astype(BF16)
+
+    def out_copy(u):
+        return pltpu.make_async_copy(stage.at[lax.rem(u, 2)], out_hbm.at[:, tile(u, UNIT)], o_sem.at[lax.rem(u, 2)])
+
+    def finish(u):
+        @pl.when(u >= 2)
+        def _():
+            out_copy(u - 2).wait()
+
+        pair = 2 * pair_cap
+        for k, q in enumerate(near_chips + [far_chip]):
+            if k == 0:
+                arrived(u, lax.rem(me + n - partner, n))
+            else:
+                arrived(u, lax.rem(me + n - 2 * q, n))
+                arrived(u, lax.rem(me + n - 2 * q - 1 + n, n))
+
+            @pl.loop(0, tok_loc // 128)
+            def _(t):
+                rows = tile(t, 128)
+                got = xb[u, pl.ds(pl.multiple_of(landing(me) + q * pair, pair), pair), :]
+                acc = hacc[rows, 0:UNIT] if k > 0 else dot(hsb[rows, :], ws2[:, tile(u, UNIT)]).astype(BF16).astype(F32)
+                for part in range(3):
+                    r0, c0 = weights_at(part)
+                    acc += dot(pick[pl.ds(pl.multiple_of(r0 + t * 128, 128), 128), pl.ds(pl.multiple_of(c0 + q * pair, pair), pair)], got)
+                if k < 3:
+                    hacc[rows, 0:UNIT] = acc
+                else:
+                    x_own = xb[u, pl.ds(pl.multiple_of(me * tok_loc + t * 128, 128), 128), :].astype(F32)
+                    stage[lax.rem(u, 2), rows, :] = (x_own + acc).astype(BF16)
+
+        out_copy(u).start()
+
+    send_back(0)
+    build_weights()
+    ws2_copy.wait()
+
+    @pl.loop(1, nu)
+    def _(u):
+        second_product(u)
+        send_back(u)
+        finish(u - 1)
+
+    finish(nu - 1)
+    out_copy(nu - 2).wait()
+    out_copy(nu - 1).wait()
+
+    @pl.loop(nu - SEND_SLOTS, nu)
+    def _(u):
+        for i in range(1, n):
+            back(u, i).wait_send()
 
 
 def solution(mesh):
@@ -421,8 +482,7 @@
                 vmem((rows_total, tokens), BF16),
                 vmem((slots, rows_total), BF16),
                 vmem((SEND_SLOTS, slots, UNIT), BF16),
-                vmem((nu, slots, UNIT), BF16),
-                vmem((rows_total, UNIT), BF16),
+                vmem((2, rows_total, UNIT), BF16),
                 vmem((rows_total, ff), F32),
                 vmem((W1_DEPTH, EXPERT_GROUP, UNIT, ff), BF16),
                 vmem((W2_DEPTH, EXPERT_GROUP, ff, UNIT), BF16),
@@ -444,7 +504,7 @@
                 vmem((n, 8, pair_cap), F32),
                 vmem((n, 8, pair_cap), F32),
                 dma((nu,)), dma((3,)), dma((n,)), dma((n,)), dma((nu, KINDS)), dma((nu, KINDS)),
-                dma((W1_DEPTH,)), dma((W2_DEPTH,)), dma((n,)), dma((n,)), dma((nu, n)), dma((nu, n)), dma((2,)),
+                dma((W1_DEPTH,)), dma((W2_DEPTH,)), dma((n,)), dma((n,)), dma((nu, n)), dma((nu, n)), dma((2,)), pltpu.SemaphoreType.REGULAR,
             ],
             compiler_params=pltpu.CompilerParams(collective_id=0, has_side_effects=True, vmem_limit_bytes=VMEM_BYTES),
             name="moe_layer",

time: 196 us -> 199 us (1.015)
  Pallas kernels: 193 us -> 196 us
    pallas_call x1, Pallas kernels: 193 us -> 196 us  [local_layer(): pl.pallas_call(functools.partial(layer_kernel, n), out_shape=jax.ShapeDty...]
where the time goes in v3:
time: 199 us
  Pallas kernels  196 us (98%)
  local copies, waits for them, and re-layouts  3.16 us (2%)
    pallas_call x1, Pallas kernels, local_layer(): pl.pallas_call(functools.partial(layer_kernel, n), out_shape=jax.ShapeDty...  196 us

profile of v3, /device:TPU:113, one launch (start us, length us, event | category | flops | bytes accessed | tf_op | source)
XLA Modules:
  0.0 199.3 jit_solution(1700946223976374872)
XLA Ops:
  0.0 196.1 %moe_layer.1 = bf16[512,2048]{1,0:T(8,128)(2,1)} custom-call(bf16[512,2048]{1,0:T(8,128)(2,1)} %x_hbm.1, f32[512,256]{1,0:T(8,128)} %lg_hbm.1, bf16[32,2048,512]{2,1,0:T(8,128)(2,1)} %w1_hbm.1, bf16[2048,512]{1,0:T(8,128)(2,1)} %ws1_hbm.1, bf16[32,512,2048]{2,1,0:T(8,128)(2,1)} %w2_hbm.1, bf16[512,2048]{1,0:T(8,128)(2,1)} %ws2_hbm.1), custom_call_target="tpu_custom_call" | custom-call | tf_op jit(solution)/shard_map/moe_layer/pallas_call | solution.py:475
  196.1 3.2 %copy.8 = bf16[512,2048]{1,0:T(8,128)(2,1)} copy(bf16[512,2048]{1,0:T(8,128)(2,1)} %moe_layer.1) | data formatting | bytes 4194304

commit v4 on v3

--- a/solution.py
+++ b/solution.py
@@ -18,6 +18,7 @@
 W1_DEPTH = 6
 W2_DEPTH = 8
 KINDS = 9
+GATHER_ROWS = 512
 
 
 def dot(a, b):
@@ -73,10 +74,6 @@
     barrier = pltpu.get_barrier_semaphore()
     for i in range(1, n):
         pl.semaphore_signal(barrier, inc=1, device_id={"ep": lax.rem(me + i, n)}, device_id_type=MESH)
-    for step in range(W1_DEPTH - 1):
-        w1_copy(step).start()
-    for step in range(W2_DEPTH - 1):
-        w2_copy(step).start()
     for cp in x_copies:
         cp.wait()
     pl.semaphore_wait(barrier, n - 1)
@@ -116,6 +113,10 @@
 
     send_own(0)
     send_own(1)
+    for step in range(W1_DEPTH - 1):
+        w1_copy(step).start()
+    for step in range(W2_DEPTH - 1):
+        w2_copy(step).start()
 
     lg_copy.wait()
     ws2_copy.start()
@@ -149,16 +150,6 @@
     forward_near(0)
     send_own(2)
 
-    ws1_copy.wait()
-
-    @pl.loop(0, tok_loc // 128)
-    def _(t):
-        rows = pl.ds(pl.multiple_of(me * tok_loc + t * 128, 128), 128)
-        acc = dot(xb[0, rows, :], ws1[0:UNIT, :])
-        for u in range(1, nu):
-            acc += dot(xb[u, rows, :], ws1[u * UNIT:(u + 1) * UNIT, :])
-        hsb[tile(t, 128), :] = gelu(acc).astype(BF16)
-
     forward_near(1)
     send_own(3)
 
@@ -202,29 +193,33 @@
             ids = lax.broadcasted_iota(jnp.int32, (128, tok_loc), 1).astype(F32) + (s * tok_loc).astype(F32)
             pick[pl.ds(g * 128, 128), tile(s, tok_loc)] = jnp.where(ids == col, 1.0, 0.0).astype(BF16)
 
-    source = jnp.floor(tok_flat * (1.0 / tok_loc))
-    loc = tok_flat - source * tok_loc
-    of_src = jnp.where(lax.broadcasted_iota(jnp.int32, (n, rows_total), 0).astype(F32) == source, 1.0, 0.0)
-    sq = (rows_total, rows_total)
-    before = jnp.where(lax.broadcasted_iota(jnp.int32, sq, 0) < lax.broadcasted_iota(jnp.int32, sq, 1), 1.0, 0.0).astype(BF16)
-    slot = jnp.sum(of_src * dot(of_src.astype(BF16), before), axis=0, keepdims=True)
-    hi = jnp.floor(loc * (1.0 / 16))
-    g_hi = gate_flat.astype(BF16).astype(F32)
-    g_mid = (gate_flat - g_hi).astype(BF16).astype(F32)
-    route[0:1, :] = hi
-    route[1:2, :] = loc - 16 * hi
-    route[2:3, :] = jnp.ones_like(hi)
-    route[3:4, :] = g_hi
-    route[4:5, :] = g_mid
-    route[5:6, :] = gate_flat - g_hi - g_mid
-    route[6:7, :] = source * pair_cap + slot
-    route[7:8, :] = jnp.zeros_like(hi)
+    route[6:7, :] = tok_flat
+    route[7:8, :] = gate_flat
 
     def meta_copy(i):
         dst = lax.rem(me + i, n)
         return pltpu.make_async_remote_copy(src_ref=metas.at[dst], dst_ref=metar.at[me], send_sem=m_ss.at[i], recv_sem=m_rs.at[i], device_id={"ep": dst}, device_id_type=MESH)
 
     def announce():
+        tok_flat, gate_flat = route[6:7, :], route[7:8, :]
+        source = jnp.floor(tok_flat * (1.0 / tok_loc))
+        loc = tok_flat - source * tok_loc
+        of_src = jnp.where(lax.broadcasted_iota(jnp.int32, (n, rows_total), 0).astype(F32) == source, 1.0, 0.0)
+        sq = (rows_total, rows_total)
+        before = jnp.where(lax.broadcasted_iota(jnp.int32, sq, 0) < lax.broadcasted_iota(jnp.int32, sq, 1), 1.0, 0.0).astype(BF16)
+        slot = jnp.sum(of_src * dot(of_src.astype(BF16), before), axis=0, keepdims=True)
+        hi = jnp.floor(loc * (1.0 / 16))
+        g_hi = gate_flat.astype(BF16).astype(F32)
+        g_mid = (gate_flat - g_hi).astype(BF16).astype(F32)
+        route[0:1, :] = hi
+        route[1:2, :] = loc - 16 * hi
+        route[2:3, :] = jnp.ones_like(hi)
+        route[3:4, :] = g_hi
+        route[4:5, :] = g_mid
+        route[5:6, :] = gate_flat - g_hi - g_mid
+        route[6:7, :] = source * pair_cap + slot
+        route[7:8, :] = jnp.zeros_like(hi)
+
         for g in range(rows_total // 128):
             key = route[6:7, g * 128:(g + 1) * 128]
 
@@ -251,20 +246,31 @@
     def gather_near(u):
         land_near(u)
 
-        @pl.loop(0, rows_total // 256)
+        @pl.loop(0, rows_total // GATHER_ROWS)
         def _(t):
-            acc = dot(pick[tile(t, 256), tile(near_chips[0], chip)], xb[u, tile(near_chips[0], chip), :])
+            rows = tile(t, GATHER_ROWS)
+            acc = dot(pick[rows, tile(near_chips[0], chip)], xb[u, tile(near_chips[0], chip), :])
             for q in near_chips[1:]:
-                acc += dot(pick[tile(t, 256), tile(q, chip)], xb[u, tile(q, chip), :])
-            xg[lax.rem(u, 2), tile(t, 256), :] = acc.astype(BF16)
+                acc += dot(pick[rows, tile(q, chip)], xb[u, tile(q, chip), :])
+            xg[lax.rem(u, 2), rows, :] = acc.astype(BF16)
 
     def gather_far(u):
         land_far(u)
 
-        @pl.loop(0, rows_total // 256)
+        @pl.loop(0, rows_total // GATHER_ROWS)
         def _(t):
-            acc = dot(pick[tile(t, 256), tile(far_chip, chip)], xb[u, tile(far_chip, chip), :])
-            xg[lax.rem(u, 2), tile(t, 256), :] = (xg[lax.rem(u, 2), tile(t, 256), :].astype(F32) + acc).astype(BF16)
+            rows = tile(t, GATHER_ROWS)
+            acc = dot(pick[rows, tile(far_chip, chip)], xb[u, tile(far_chip, chip), :])
+            xg[lax.rem(u, 2), rows, :] = (xg[lax.rem(u, 2), rows, :].astype(F32) + acc).astype(BF16)
+
+    def gather(u):
+        land_near(u)
+        land_far(u)
+
+        @pl.loop(0, rows_total // GATHER_ROWS)
+        def _(t):
+            rows = tile(t, GATHER_ROWS)
+            xg[lax.rem(u, 2), rows, :] = dot(pick[rows, :], xb[u]).astype(BF16)
 
     def next_w1(step):
         @pl.when(step + W1_DEPTH - 1 < steps)
@@ -290,18 +296,15 @@
                 rows = tile(g * EXPERT_GROUP + i, cap)
                 hacc[rows, :] += dot(xg[lax.rem(u, 2), rows, :], w1buf[buf, i])
 
+    forward_near(2)
+    send_own(4)
     forward_far(0)
-
-    @pl.loop(2, 4)
-    def _(u):
-        forward_near(u)
-        send_own(u + 2)
-        gather_near(u - 2)
-        gather_far(u - 2)
-        forward_far(u - 1)
-        first_product(u - 2, 0, groups)
-
-    @pl.loop(4, nu)
+    gather(0)
+    first_product(0, 0, groups)
+    forward_far(1)
+    gather(1)
+
+    @pl.loop(3, nu - 1)
     def _(u):
         forward_near(u)
 
@@ -309,25 +312,22 @@
         def _():
             send_own(u + 2)
 
+        first_product(u - 2, 0, groups)
+        forward_far(u - 1)
+        gather(u - 1)
+
         @pl.when(u == 4)
         def _():
-            gather_near(2)
-            gather_far(2)
-            first_product(2, 0, groups)
             announce()
-            gather_near(3)
-
-        gather_near(u)
-        forward_far(u - 1)
-        gather_far(u - 1)
-        first_product(u - 1, 0, groups // 2)
-
-        @pl.when(u == nu - 1)
-        def _():
-            forward_far(nu - 1)
-
-        first_product(u - 1, groups // 2, groups)
-
+
+    first_product(nu - 3, 0, groups)
+    gather_near(nu - 2)
+    forward_near(nu - 1)
+    forward_far(nu - 2)
+    gather_near(nu - 1)
+    gather_far(nu - 2)
+    forward_far(nu - 1)
+    first_product(nu - 2, 0, groups)
     gather_far(nu - 1)
 
     @pl.loop(0, nu)
@@ -382,12 +382,18 @@
             for i in range(1, n):
                 back(u - SEND_SLOTS, i).wait_send()
 
-        @pl.loop(1, n)
-        def _(i):
-            rows = tile(lax.rem(me + i, n), pair_cap)
-            sendb[lax.rem(u, SEND_SLOTS), rows, :] = dot(sel[rows, :], z[...]).astype(BF16)
-            back(u, i).start()
-
+        pair = 2 * pair_cap
+        chip_me = me // 2
+
+        @pl.loop(1, n // 2)
+        def _(k):
+            q = lax.rem(chip_me + k, n // 2)
+            sendb[lax.rem(u, SEND_SLOTS), tile(q, pair), :] = dot(sel[tile(q, pair), :], z[...]).astype(BF16)
+            back(u, lax.rem(2 * q - me + n, n)).start()
+            back(u, lax.rem(2 * q + 1 - me + n, n)).start()
+
+        sendb[lax.rem(u, SEND_SLOTS), tile(partner, pair_cap), :] = dot(sel[tile(partner, pair_cap), :], z[...]).astype(BF16)
+        back(u, lax.rem(partner - me + n, n)).start()
         xb[u, pl.ds(pl.multiple_of(landing(me) + me * pair_cap, pair_cap), pair_cap), :] = dot(sel[tile(me, pair_cap), :], z[...]).astype(BF16)
 
     def weights_at(k):
@@ -408,38 +414,72 @@
     def out_copy(u):
         return pltpu.make_async_copy(stage.at[lax.rem(u, 2)], out_hbm.at[:, tile(u, UNIT)], o_sem.at[lax.rem(u, 2)])
 
-    def finish(u):
+    def finish(u, last=False):
         @pl.when(u >= 2)
         def _():
             out_copy(u - 2).wait()
 
         pair = 2 * pair_cap
-        for k, q in enumerate(near_chips + [far_chip]):
-            if k == 0:
-                arrived(u, lax.rem(me + n - partner, n))
-            else:
-                arrived(u, lax.rem(me + n - 2 * q, n))
-                arrived(u, lax.rem(me + n - 2 * q - 1 + n, n))
-
+
+        def shared(rows):
+            return dot(hsb[rows, :], ws2[:, tile(u, UNIT)]).astype(BF16).astype(F32)
+
+        def weighted(t, acc, q):
+            for part in range(3):
+                r0, c0 = weights_at(part)
+                lhs_rows = pl.ds(pl.multiple_of(r0 + t * 128, 128), 128)
+                if q is None:
+                    acc += dot(pick[lhs_rows, c0:c0 + slots], xb[u, pl.ds(pl.multiple_of(landing(me), slots), slots), :])
+                else:
+                    acc += dot(pick[lhs_rows, pl.ds(pl.multiple_of(c0 + q * pair, pair), pair)], xb[u, pl.ds(pl.multiple_of(landing(me) + q * pair, pair), pair), :])
+            return acc
+
+        def write(t, acc):
+            x_own = xb[u, pl.ds(pl.multiple_of(me * tok_loc + t * 128, 128), 128), :].astype(F32)
+            stage[lax.rem(u, 2), tile(t, 128), :] = (x_own + acc).astype(BF16)
+
+        def chip_arrived(q):
+            arrived(u, lax.rem(me + n - 2 * q, n))
+            arrived(u, lax.rem(me + n - 2 * q - 1 + n, n))
+
+        arrived(u, lax.rem(me + n - partner, n))
+        chip_arrived(near_chips[1])
+        chip_arrived(near_chips[2])
+        if last:
             @pl.loop(0, tok_loc // 128)
             def _(t):
-                rows = tile(t, 128)
-                got = xb[u, pl.ds(pl.multiple_of(landing(me) + q * pair, pair), pair), :]
-                acc = hacc[rows, 0:UNIT] if k > 0 else dot(hsb[rows, :], ws2[:, tile(u, UNIT)]).astype(BF16).astype(F32)
-                for part in range(3):
-                    r0, c0 = weights_at(part)
-                    acc += dot(pick[pl.ds(pl.multiple_of(r0 + t * 128, 128), 128), pl.ds(pl.multiple_of(c0 + q * pair, pair), pair)], got)
-                if k < 3:
-                    hacc[rows, 0:UNIT] = acc
-                else:
-                    x_own = xb[u, pl.ds(pl.multiple_of(me * tok_loc + t * 128, 128), 128), :].astype(F32)
-                    stage[lax.rem(u, 2), rows, :] = (x_own + acc).astype(BF16)
+                acc = shared(tile(t, 128))
+                for q in near_chips:
+                    acc = weighted(t, acc, q)
+                hacc[tile(t, 128), 0:UNIT] = acc
+
+            chip_arrived(far_chip)
+
+            @pl.loop(0, tok_loc // 128)
+            def _(t):
+                write(t, weighted(t, hacc[tile(t, 128), 0:UNIT], far_chip))
+        else:
+            chip_arrived(far_chip)
+
+            @pl.loop(0, tok_loc // 128)
+            def _(t):
+                write(t, weighted(t, shared(tile(t, 128)), None))
 
         out_copy(u).start()
 
     send_back(0)
     build_weights()
+    ws1_copy.wait()
     ws2_copy.wait()
+
+    @pl.loop(0, tok_loc // 128)
+    def _(t):
+        rows = pl.ds(pl.multiple_of(me * tok_loc + t * 128, 128), 128)
+        acc = dot(xb[0, rows, :], ws1[0:UNIT, :])
+        for u in range(1, nu):
+            acc += dot(xb[u, rows, :], ws1[u * UNIT:(u + 1) * UNIT, :])
+        hsb[tile(t, 128), :] = gelu(acc).astype(BF16)
+
 
     @pl.loop(1, nu)
     def _(u):
@@ -447,7 +487,7 @@
         send_back(u)
         finish(u - 1)
 
-    finish(nu - 1)
+    finish(nu - 1, True)
     out_copy(nu - 2).wait()
     out_copy(nu - 1).wait()
 

time: 199 us -> 192 us (0.965)
  Pallas kernels: 196 us -> 188 us
    pallas_call x1, Pallas kernels: 196 us -> 188 us  [local_layer(): pl.pallas_call(functools.partial(layer_kernel, n), out_shape=jax.ShapeDty...]
where the time goes in v4:
time: 192 us; the launch traced here: 191 us
  Pallas kernels  188 us (98%)
  local copies, waits for them, and re-layouts  3.16 us (2%)
    pallas_call x1, Pallas kernels, local_layer(): pl.pallas_call(functools.partial(layer_kernel, n), out_shape=jax.ShapeDty...  188 us

profile of v4, /device:TPU:113, one launch (start us, length us, event | category | flops | bytes accessed | tf_op | source)
XLA Modules:
  0.0 191.5 jit_solution(6438867663021515115)
XLA Ops:
  0.0 188.3 %moe_layer.1 = bf16[512,2048]{1,0:T(8,128)(2,1)} custom-call(bf16[512,2048]{1,0:T(8,128)(2,1)} %x_hbm.1, f32[512,256]{1,0:T(8,128)} %lg_hbm.1, bf16[32,2048,512]{2,1,0:T(8,128)(2,1)} %w1_hbm.1, bf16[2048,512]{1,0:T(8,128)(2,1)} %ws1_hbm.1, bf16[32,512,2048]{2,1,0:T(8,128)(2,1)} %w2_hbm.1, bf16[512,2048]{1,0:T(8,128)(2,1)} %ws2_hbm.1), custom_call_target="tpu_custom_call" | custom-call | tf_op jit(solution)/shard_map/moe_layer/pallas_call | solution.py:515
  188.3 3.2 %copy.8 = bf16[512,2048]{1,0:T(8,128)(2,1)} copy(bf16[512,2048]{1,0:T(8,128)(2,1)} %moe_layer.1) | data formatting | bytes 4194304

commit v5 on v4

--- a/solution.py
+++ b/solution.py
@@ -11,12 +11,12 @@
 MESH = pl.DeviceIdType.MESH
 F32 = jnp.float32
 BF16 = jnp.bfloat16
-VMEM_BYTES = 64 * 1024 * 1024 - 65536
-EXPERT_GROUP = 4
+VMEM_BYTES = 60 * 1024 * 1024
+EXPERT_GROUP = 8
 UNIT = 256
 SEND_SLOTS = 3
-W1_DEPTH = 6
-W2_DEPTH = 8
+W1_DEPTH = 4
+W2_DEPTH = 4
 KINDS = 9
 GATHER_ROWS = 512
 
@@ -33,10 +33,10 @@
     return pl.ds(pl.multiple_of(i * size, size), size)
 
 
-def layer_kernel(n, x_hbm, lg_hbm, w1_hbm, ws1_hbm, w2_hbm, ws2_hbm, out_hbm,
-                 xb, pick, sel, sendb, xg, hacc, w1buf, w2buf, z, h, hsb, ws1, ws2, stage,
+def layer_kernel(n, x_hbm, lg_hbm, w1_hbm, ws1_hbm, w2_hbm, ws2_hbm, out_ref,
+                 xb, pick, sel, sendb, xg, hacc, w1buf, w2buf, z, h, hsb, ws1, ws2,
                  sc, gate_p, cand, cand_t, cand_r, m_sc, m_tok, m_gate, route, metas, metar,
-                 x_sem, in_sem, c_ss, c_rs, ss, rs, w1_sem, w2_sem, m_ss, m_rs, a_ss, a_rs, o_sem, free_sem):
+                 x_sem, in_sem, c_ss, c_rs, ss, rs, w1_sem, w2_sem, m_ss, m_rs, a_ss, a_rs, free_sem):
     me = lax.axis_index("ep")
     core = lax.rem(me, 2)
     partner = me + 1 - 2 * core
@@ -126,15 +126,17 @@
     cand[...] = jnp.zeros_like(cand)
     tok_iota = lax.broadcasted_iota(jnp.int32, sc.shape, 0).astype(F32)
 
-    @pl.loop(0, cap)
-    def _(j):
+    def best_local(j, top):
         cur = sc[...]
-        top = jnp.max(cur, axis=0, keepdims=True)
         hit = cur == top
         cand[pl.ds(j, 1), :] = top
         cand[pl.ds(cap + j, 1), :] = jnp.sum(jnp.where(hit, tok_iota, 0.0), axis=0, keepdims=True)
         cand[pl.ds(2 * cap + j, 1), :] = jnp.sum(jnp.where(hit, gate_p[...], 0.0), axis=0, keepdims=True)
-        sc[...] = jnp.where(hit, -jnp.inf, cur)
+        cur = jnp.where(hit, -jnp.inf, cur)
+        sc[...] = cur
+        return jnp.max(cur, axis=0, keepdims=True)
+
+    lax.fori_loop(0, cap, best_local, jnp.max(raw, axis=0, keepdims=True))
 
     flat_t = cand[...].T
     for d in range(n):
@@ -321,8 +323,8 @@
             announce()
 
     first_product(nu - 3, 0, groups)
+    forward_near(nu - 1)
     gather_near(nu - 2)
-    forward_near(nu - 1)
     forward_far(nu - 2)
     gather_near(nu - 1)
     gather_far(nu - 2)
@@ -411,14 +413,7 @@
                 r0, c0 = weights_at(k)
                 pick[pl.ds(r0, tok_loc), pl.ds(pl.multiple_of(c0 + o * pair_cap, pair_cap), pair_cap)] = jnp.where(hit, metar[o, 3 + k:4 + k, :], 0.0).astype(BF16)
 
-    def out_copy(u):
-        return pltpu.make_async_copy(stage.at[lax.rem(u, 2)], out_hbm.at[:, tile(u, UNIT)], o_sem.at[lax.rem(u, 2)])
-
     def finish(u, last=False):
-        @pl.when(u >= 2)
-        def _():
-            out_copy(u - 2).wait()
-
         pair = 2 * pair_cap
 
         def shared(rows):
@@ -436,7 +431,7 @@
 
         def write(t, acc):
             x_own = xb[u, pl.ds(pl.multiple_of(me * tok_loc + t * 128, 128), 128), :].astype(F32)
-            stage[lax.rem(u, 2), tile(t, 128), :] = (x_own + acc).astype(BF16)
+            out_ref[tile(t, 128), tile(u, UNIT)] = (x_own + acc).astype(BF16)
 
         def chip_arrived(q):
             arrived(u, lax.rem(me + n - 2 * q, n))
@@ -465,7 +460,6 @@
             def _(t):
                 write(t, weighted(t, shared(tile(t, 128)), None))
 
-        out_copy(u).start()
 
     send_back(0)
     build_weights()
@@ -488,8 +482,6 @@
         finish(u - 1)
 
     finish(nu - 1, True)
-    out_copy(nu - 2).wait()
-    out_copy(nu - 1).wait()
 
     @pl.loop(nu - SEND_SLOTS, nu)
     def _(u):
@@ -514,9 +506,9 @@
         vmem = pltpu.VMEM
         return pl.pallas_call(
             functools.partial(layer_kernel, n),
-            out_shape=jax.ShapeDtypeStruct((tok_loc, d_model), BF16),
+            out_shape=pltpu.VMEM((tok_loc, d_model), BF16),
             in_specs=[hbm] * 6,
-            out_specs=hbm,
+            out_specs=pl.BlockSpec(memory_space=pltpu.VMEM),
             scratch_shapes=[
                 vmem((nu, tokens, UNIT), BF16),
                 vmem((rows_total, tokens), BF16),
@@ -531,7 +523,6 @@
                 vmem((tok_loc, shared_in.shape[1]), BF16),
                 vmem(shared_in.shape, BF16),
                 vmem(shared_out.shape, BF16),
-                vmem((2, tok_loc, UNIT), BF16),
                 vmem((tok_loc, experts), F32),
                 vmem((tok_loc, experts), F32),
                 vmem((128, experts), F32),
@@ -544,7 +535,7 @@
                 vmem((n, 8, pair_cap), F32),
                 vmem((n, 8, pair_cap), F32),
                 dma((nu,)), dma((3,)), dma((n,)), dma((n,)), dma((nu, KINDS)), dma((nu, KINDS)),
-                dma((W1_DEPTH,)), dma((W2_DEPTH,)), dma((n,)), dma((n,)), dma((nu, n)), dma((nu, n)), dma((2,)), pltpu.SemaphoreType.REGULAR,
+                dma((W1_DEPTH,)), dma((W2_DEPTH,)), dma((n,)), dma((n,)), dma((nu, n)), dma((nu, n)), pltpu.SemaphoreType.REGULAR,
             ],
             compiler_params=pltpu.CompilerParams(collective_id=0, has_side_effects=True, vmem_limit_bytes=VMEM_BYTES),
             name="moe_layer",

time: 192 us -> 184 us (0.958)
  Pallas kernels: 188 us -> 183 us
    pallas_call x1, Pallas kernels: 188 us -> 183 us  [local_layer(): pl.pallas_call(functools.partial(layer_kernel, n), out_shape=pltpu.VMEM((...]
where the time goes in v5:
time: 184 us
  Pallas kernels  183 us (99%)
    pallas_call x1, Pallas kernels, local_layer(): pl.pallas_call(functools.partial(layer_kernel, n), out_shape=pltpu.VMEM((...  183 us

profile of v5, /device:TPU:113, one launch (start us, length us, event | category | flops | bytes accessed | tf_op | source)
XLA Modules:
  0.0 184.1 jit_solution(11934277255106747468)
XLA Ops:
  0.0 182.8 %moe_layer.1 = bf16[512,2048]{1,0:T(8,128)(2,1)S(1)} custom-call(bf16[512,2048]{1,0:T(8,128)(2,1)} %x_hbm.1, f32[512,256]{1,0:T(8,128)} %lg_hbm.1, bf16[32,2048,512]{2,1,0:T(8,128)(2,1)} %w1_hbm.1, bf16[2048,512]{1,0:T(8,128)(2,1)} %ws1_hbm.1, bf16[32,512,2048]{2,1,0:T(8,128)(2,1)} %w2_hbm.1, bf16[512,2048]{1,0:T(8,128)(2,1)} %ws2_hbm.1), custom_call_target="tpu_custom_call" | custom-call | tf_op jit(solution)/shard_map/moe_layer/pallas_call | solution.py:507
  182.8 1.3 copy.8

commit v6 on v5

--- a/solution.py
+++ b/solution.py
@@ -15,9 +15,10 @@
 EXPERT_GROUP = 8
 UNIT = 256
 SEND_SLOTS = 3
-W1_DEPTH = 4
+W1_DEPTH = 5
 W2_DEPTH = 4
 KINDS = 9
+COMBINE_ROWS = 256
 GATHER_ROWS = 512
 
 
@@ -34,7 +35,7 @@
 
 
 def layer_kernel(n, x_hbm, lg_hbm, w1_hbm, ws1_hbm, w2_hbm, ws2_hbm, out_ref,
-                 xb, pick, sel, sendb, xg, hacc, w1buf, w2buf, z, h, hsb, ws1, ws2,
+                 xb, pick, sel, sendb, xg, hacc, w1buf, w2buf, z, h, hsb, ws2,
                  sc, gate_p, cand, cand_t, cand_r, m_sc, m_tok, m_gate, route, metas, metar,
                  x_sem, in_sem, c_ss, c_rs, ss, rs, w1_sem, w2_sem, m_ss, m_rs, a_ss, a_rs, free_sem):
     me = lax.axis_index("ep")
@@ -67,9 +68,8 @@
     own = tile(me, tok_loc)
     x_copies = [pltpu.make_async_copy(x_hbm.at[:, pl.ds(u * UNIT, UNIT)], xb.at[u, own], x_sem.at[u]) for u in range(nu)]
     lg_copy = pltpu.make_async_copy(lg_hbm, sc, in_sem.at[0])
-    ws1_copy = pltpu.make_async_copy(ws1_hbm, ws1, in_sem.at[1])
     ws2_copy = pltpu.make_async_copy(ws2_hbm, ws2, in_sem.at[2])
-    for cp in x_copies + [lg_copy, ws1_copy]:
+    for cp in x_copies + [lg_copy]:
         cp.start()
     barrier = pltpu.get_barrier_semaphore()
     for i in range(1, n):
@@ -298,42 +298,7 @@
                 rows = tile(g * EXPERT_GROUP + i, cap)
                 hacc[rows, :] += dot(xg[lax.rem(u, 2), rows, :], w1buf[buf, i])
 
-    forward_near(2)
-    send_own(4)
-    forward_far(0)
-    gather(0)
-    first_product(0, 0, groups)
-    forward_far(1)
-    gather(1)
-
-    @pl.loop(3, nu - 1)
-    def _(u):
-        forward_near(u)
-
-        @pl.when(u + 2 < nu)
-        def _():
-            send_own(u + 2)
-
-        first_product(u - 2, 0, groups)
-        forward_far(u - 1)
-        gather(u - 1)
-
-        @pl.when(u == 4)
-        def _():
-            announce()
-
-    first_product(nu - 3, 0, groups)
-    forward_near(nu - 1)
-    gather_near(nu - 2)
-    forward_far(nu - 2)
-    gather_near(nu - 1)
-    gather_far(nu - 2)
-    forward_far(nu - 1)
-    first_product(nu - 2, 0, groups)
-    gather_far(nu - 1)
-
-    @pl.loop(0, nu)
-    def _(u):
+    def drain(u):
         hop(u, 0, me, None, right).wait_send()
         hop(u, 1, me, None, left).wait_send()
         hop(u, 2, me, None, partner).wait_send()
@@ -344,6 +309,45 @@
         hop(u, 7, far, 0, partner).wait_send()
         hop(u, 8, far, 1, partner).wait_send()
 
+    forward_near(2)
+    send_own(4)
+    forward_far(0)
+    gather(0)
+    first_product(0, 0, groups)
+    forward_far(1)
+    gather(1)
+
+    @pl.loop(3, nu - 1)
+    def _(u):
+        forward_near(u)
+
+        @pl.when(u + 2 < nu)
+        def _():
+            send_own(u + 2)
+
+        first_product(u - 2, 0, groups)
+        drain(u - 3)
+        forward_far(u - 1)
+        gather(u - 1)
+
+        @pl.when(u == 4)
+        def _():
+            announce()
+
+    first_product(nu - 3, 0, groups)
+    forward_near(nu - 1)
+    gather_near(nu - 2)
+    drain(nu - 4)
+    drain(nu - 3)
+    forward_far(nu - 2)
+    gather_near(nu - 1)
+    gather_far(nu - 2)
+    forward_far(nu - 1)
+    first_product(nu - 2, 0, groups)
+    drain(nu - 2)
+    gather_far(nu - 1)
+
+    drain(nu - 1)
     for i in range(1, n):
         pl.semaphore_signal(free_sem, inc=1, device_id={"ep": lax.rem(me + i, n)}, device_id_type=MESH)
 
@@ -356,6 +360,9 @@
             h[rows, :] = act
             z[rows, :] = dot(act, w2buf[buf2, i]).astype(BF16)
 
+    ws1_copies = [pltpu.make_async_copy(ws1_hbm.at[pl.ds(u * UNIT, UNIT), :], w1buf.at[0, u], x_sem.at[u]) for u in range(nu)]
+    for cp in ws1_copies:
+        cp.start()
     pl.semaphore_wait(free_sem, n - 1)
 
     def landing(d):
@@ -387,8 +394,7 @@
         pair = 2 * pair_cap
         chip_me = me // 2
 
-        @pl.loop(1, n // 2)
-        def _(k):
+        for k in (1, n // 2 - 1, 2):
             q = lax.rem(chip_me + k, n // 2)
             sendb[lax.rem(u, SEND_SLOTS), tile(q, pair), :] = dot(sel[tile(q, pair), :], z[...]).astype(BF16)
             back(u, lax.rem(2 * q - me + n, n)).start()
@@ -422,7 +428,7 @@
         def weighted(t, acc, q):
             for part in range(3):
                 r0, c0 = weights_at(part)
-                lhs_rows = pl.ds(pl.multiple_of(r0 + t * 128, 128), 128)
+                lhs_rows = pl.ds(pl.multiple_of(r0 + t * COMBINE_ROWS, COMBINE_ROWS), COMBINE_ROWS)
                 if q is None:
                     acc += dot(pick[lhs_rows, c0:c0 + slots], xb[u, pl.ds(pl.multiple_of(landing(me), slots), slots), :])
                 else:
@@ -430,8 +436,8 @@
             return acc
 
         def write(t, acc):
-            x_own = xb[u, pl.ds(pl.multiple_of(me * tok_loc + t * 128, 128), 128), :].astype(F32)
-            out_ref[tile(t, 128), tile(u, UNIT)] = (x_own + acc).astype(BF16)
+            x_own = xb[u, pl.ds(pl.multiple_of(me * tok_loc + t * COMBINE_ROWS, COMBINE_ROWS), COMBINE_ROWS), :].astype(F32)
+            out_ref[tile(t, COMBINE_ROWS), tile(u, UNIT)] = (x_own + acc).astype(BF16)
 
         def chip_arrived(q):
             arrived(u, lax.rem(me + n - 2 * q, n))
@@ -441,37 +447,38 @@
         chip_arrived(near_chips[1])
         chip_arrived(near_chips[2])
         if last:
-            @pl.loop(0, tok_loc // 128)
+            @pl.loop(0, tok_loc // COMBINE_ROWS)
             def _(t):
-                acc = shared(tile(t, 128))
+                acc = shared(tile(t, COMBINE_ROWS))
                 for q in near_chips:
                     acc = weighted(t, acc, q)
-                hacc[tile(t, 128), 0:UNIT] = acc
+                hacc[tile(t, COMBINE_ROWS), 0:UNIT] = acc
 
             chip_arrived(far_chip)
 
-            @pl.loop(0, tok_loc // 128)
+            @pl.loop(0, tok_loc // COMBINE_ROWS)
             def _(t):
-                write(t, weighted(t, hacc[tile(t, 128), 0:UNIT], far_chip))
+                write(t, weighted(t, hacc[tile(t, COMBINE_ROWS), 0:UNIT], far_chip))
         else:
             chip_arrived(far_chip)
 
-            @pl.loop(0, tok_loc // 128)
+            @pl.loop(0, tok_loc // COMBINE_ROWS)
             def _(t):
-                write(t, weighted(t, shared(tile(t, 128)), None))
+                write(t, weighted(t, shared(tile(t, COMBINE_ROWS)), None))
 
 
     send_back(0)
     build_weights()
-    ws1_copy.wait()
+    for cp in ws1_copies:
+        cp.wait()
     ws2_copy.wait()
 
     @pl.loop(0, tok_loc // 128)
     def _(t):
         rows = pl.ds(pl.multiple_of(me * tok_loc + t * 128, 128), 128)
-        acc = dot(xb[0, rows, :], ws1[0:UNIT, :])
+        acc = dot(xb[0, rows, :], w1buf[0, 0])
         for u in range(1, nu):
-            acc += dot(xb[u, rows, :], ws1[u * UNIT:(u + 1) * UNIT, :])
+            acc += dot(xb[u, rows, :], w1buf[0, u])
         hsb[tile(t, 128), :] = gelu(acc).astype(BF16)
 
 
@@ -521,7 +528,6 @@
                 vmem((rows_total, UNIT), BF16),
                 vmem((rows_total, ff), BF16),
                 vmem((tok_loc, shared_in.shape[1]), BF16),
-                vmem(shared_in.shape, BF16),
                 vmem(shared_out.shape, BF16),
                 vmem((tok_loc, experts), F32),
                 vmem((tok_loc, experts), F32),

time: 184 us -> 182 us (0.989)
  Pallas kernels: 183 us -> 181 us
    pallas_call x1, Pallas kernels: 183 us -> 181 us  [local_layer(): pl.pallas_call(functools.partial(layer_kernel, n), out_shape=pltpu.VMEM((...]
where the time goes in v6:
time: 182 us
  Pallas kernels  181 us (99%)
    pallas_call x1, Pallas kernels, local_layer(): pl.pallas_call(functools.partial(layer_kernel, n), out_shape=pltpu.VMEM((...  181 us

profile of v6, /device:TPU:113, one launch (start us, length us, event | category | flops | bytes accessed | tf_op | source)
XLA Modules:
  0.0 182.0 jit_solution(1948172883995427055)
XLA Ops:
  0.0 180.6 %moe_layer.1 = bf16[512,2048]{1,0:T(8,128)(2,1)S(1)} custom-call(bf16[512,2048]{1,0:T(8,128)(2,1)} %x_hbm.1, f32[512,256]{1,0:T(8,128)} %lg_hbm.1, bf16[32,2048,512]{2,1,0:T(8,128)(2,1)} %w1_hbm.1, bf16[2048,512]{1,0:T(8,128)(2,1)} %ws1_hbm.1, bf16[32,512,2048]{2,1,0:T(8,128)(2,1)} %w2_hbm.1, bf16[512,2048]{1,0:T(8,128)(2,1)} %ws2_hbm.1), custom_call_target="tpu_custom_call" | custom-call | tf_op jit(solution)/shard_map/moe_layer/pallas_call | solution.py:514
  180.6 1.3 copy.8
